TPU v7x, 32 devices: a whole 2x2x4 slice. The times are simulated.
32 devices in a mesh: gy: 4 (over z), gx: 8 (over y, x, core).
Axes of the slice: x: 2, y: 2, z: 4, core: 2. Of those that a mesh axis runs over, the one named last changes fastest.
Arguments:
- height: float32 [384, 512], P('gx', 'gy'), may hold values from -6 to 6
- east_speed: float32 [384, 512], P('gx', 'gy'), may hold values from -3 to 3
- north_speed: float32 [384, 512], P('gx', 'gy'), may hold values from -3 to 3
- water_depth: float32 [384, 512], P('gx', 'gy'), may hold values from 0.5 to 2
- ocean_mask: int32 [384, 512], P('gx', 'gy'), may hold values 0 or 1
- fold_partner: int32 [8], replicated, may hold values from 0 to 7, each once
- love_factor: float32 [360], replicated, may hold values from 0.1 to 1
Outputs:
- sal_field: float32 [384, 512], P('gx', 'gy')
- east_next: float32 [384, 512], P('gx', 'gy')
- north_next: float32 [384, 512], P('gx', 'gy')
- height_next: float32 [384, 512], P('gx', 'gy')
Inputs may be any that keep to these rules, and one draw needn't show every extreme that they name: `fold_partner`: a permutation of the tile columns.
All inputs are finite; a program needn't handle non-finite values. No bound on the sum of `ocean_mask` on one device may be relied on, other than what follows from the above.
Results may differ from a plain program's by a relative error of at most 0.00055.
Values sent between devices are 32-bit elements; how exact they have to be, the bound alone decides.
No kernel may reach another device: no remote copies, remote signals or barrier semaphores. Data moves between devices by JAX's collectives and lax.ppermute only.
A program may use at most 64 MiB of HBM per device.

v0:
```python
import math

import jax
import jax.numpy as jnp
from jax import lax
from jax.sharding import PartitionSpec as P

COURANT = 0.35


def with_halo(shard, sides, width):
    for axis, dim in sides:
        size, length = (lax.axis_size(axis), shard.shape[dim])
        up = [(i, (i + 1) % size) for i in range(size)]
        down = [(j, i) for i, j in up]
        last = lax.slice_in_dim(shard, length - width, length, axis=dim)
        first = lax.slice_in_dim(shard, 0, width, axis=dim)
        before = lax.ppermute(last, axis, up)
        after = lax.ppermute(first, axis, down)
        shard = jnp.concatenate([before, shard, after], axis=dim)
    return shard


def latitude_rows(number, lat_total, lon_total):
    rows_float = jnp.arange(number, dtype=jnp.int32).astype(jnp.float32)
    colatitude = math.pi * (rows_float + 0.5) / lat_total
    sines = jnp.sin(colatitude)
    quadrature = math.pi / lat_total * (2.0 * math.pi / lon_total) * sines
    return (jnp.cos(colatitude), sines, quadrature)


def seed_for_orders(sines, order_ints, slot_count):
    factors = jnp.arange(1, slot_count, dtype=jnp.float32)
    increments = 0.5 * jnp.log((2.0 * factors + 1.0) / (2.0 * factors))
    seed_logs = jnp.concatenate([jnp.zeros((1,), jnp.float32), jnp.cumsum(increments)])
    table_index = jnp.arange(slot_count, dtype=jnp.int32)
    picked = jnp.sum(
        jnp.where(table_index[:, None] == order_ints[None, :], seed_logs[:, None], 0.0), axis=0
    )
    exponent = order_ints.astype(jnp.float32)[None, :] * jnp.log(sines)[:, None] + picked[None, :]
    log_shift = jnp.clip(-exponent - 80.0, 0.0, 80.0)
    return (jnp.exp(exponent + log_shift) * (1.0 / math.sqrt(4.0 * math.pi)), jnp.exp(-log_shift))


def order_of_slots(first_slot, count, per_device, devices_all):
    slots = first_slot + jnp.arange(count, dtype=jnp.int32)
    owner = slots // per_device
    within = slots % per_device
    return within * devices_all + jnp.where(within % 2 == 0, owner, devices_all - 1 - owner)


def legendre_next(carry, degree, cosines, seed_rows, orders):
    previous, before = carry
    degree_value = degree.astype(jnp.float32)
    below_value = degree_value - 1.0
    growth = jnp.sqrt(
        jnp.maximum(4.0 * degree_value * degree_value - 1.0, 1.0)
        / jnp.maximum(degree_value * degree_value - orders * orders, 1.0)
    )
    damping = jnp.sqrt(
        jnp.maximum(below_value * below_value - orders * orders, 0.0)
        / jnp.maximum(4.0 * below_value * below_value - 1.0, 1.0)
    )
    stepped = growth[None, :] * (cosines[:, None] * previous - damping[None, :] * before)
    values = jnp.where(
        degree_value == orders[None, :],
        seed_rows,
        jnp.where(degree_value > orders[None, :], stepped, 0.0),
    )
    return ((values, previous), values)


def partner_rows(all_rows, fold_partner, lon_index, tile_lon):
    offset = fold_partner[lon_index] * tile_lon
    chosen = lax.dynamic_slice_in_dim(all_rows, offset, tile_lon, 1)
    return chosen[:, ::-1]


def with_north(extended, fold_values, is_top):
    channels = fold_values.shape[0]
    north_rim = extended[:channels, 1:-1, -1]
    return extended.at[:channels, 1:-1, -1].set(jnp.where(is_top, fold_values, north_rim))


def on_device(height, east_speed, north_speed, water_depth, ocean_mask, fold_partner, love_factor):
    tile_lon, tile_lat = height.shape
    degrees = love_factor.shape[0]
    lon_devices = lax.axis_size("gx")
    lat_devices = lax.axis_size("gy")
    lon_index = lax.axis_index("gx")
    lat_index = lax.axis_index("gy")
    lon_count = tile_lon * lon_devices
    lat_count = tile_lat * lat_devices
    is_top = lat_index == lat_devices - 1
    wet_cells = ocean_mask.astype(jnp.float32)
    surface = wet_cells * height
    devices_all = lon_devices * lat_devices
    per_device = (degrees + devices_all - 1) // devices_all
    slot_count = per_device * devices_all
    tile_columns = lon_index * tile_lon + jnp.arange(tile_lon, dtype=jnp.int32)

    def order_trig(first_slot, count):
        slot_orders = order_of_slots(first_slot, count, per_device, devices_all)
        phases = tile_columns[:, None] * slot_orders[None, :] % lon_count
        angles = phases.astype(jnp.float32) * (2.0 * math.pi / lon_count)
        return (jnp.cos(angles), jnp.sin(angles))

    cos_cols, sin_cols = order_trig(jnp.int32(0), slot_count // lon_devices * lax.axis_size("gx"))
    cos_rows = lax.dot_general(
        cos_cols,
        surface,
        (((0,), (0,)), ((), ())),
        precision=lax.Precision.HIGHEST,
        preferred_element_type=jnp.float32,
    )
    sin_rows = lax.dot_general(
        sin_cols,
        surface,
        (((0,), (0,)), ((), ())),
        precision=lax.Precision.HIGHEST,
        preferred_element_type=jnp.float32,
    )
    order_sums = lax.psum_scatter(
        jnp.stack([cos_rows, sin_rows], axis=1), "gx", scatter_dimension=0, tiled=True
    )
    by_order = lax.all_to_all(order_sums, "gy", split_axis=0, concat_axis=2, tiled=True)
    my_first = (lon_index * lat_devices + lat_index) * per_device
    my_order_ints = order_of_slots(my_first, per_device, per_device, devices_all)
    my_orders = my_order_ints.astype(jnp.float32)
    all_cosines, all_sines, all_weights = latitude_rows(lat_count, lat_count, lon_count)
    order_seeds, order_unscale = seed_for_orders(all_sines, my_order_ints, slot_count)
    order_empty = jnp.zeros((lat_count, per_device), jnp.float32)

    def order_advance(carry, degree):
        return legendre_next(carry, degree, all_cosines, order_seeds, my_orders)

    order_done, order_scaled_legendre = lax.scan(
        order_advance, (order_empty, order_empty), jnp.arange(degrees, dtype=jnp.int32)
    )
    order_legendre = order_scaled_legendre * order_unscale[None]
    order_weighted = by_order * all_weights[None, None, :]
    order_spectrum = jnp.einsum(
        "ljs,scj->cls", order_legendre, order_weighted, precision=lax.Precision.HIGHEST
    )
    order_mult = jnp.where(my_order_ints == 0, 1.0, 2.0).astype(jnp.float32)
    order_scaled = order_spectrum * love_factor[None, :, None] * order_mult[None, None, :]
    order_grid = jnp.einsum(
        "cls,ljs->scj", order_scaled, order_legendre, precision=lax.Precision.HIGHEST
    )
    returned = lax.all_to_all(order_grid, "gy", split_axis=2, concat_axis=0, tiled=True)
    piece = lax.all_gather(returned, "gx", axis=0, tiled=True)
    cos_cols, sin_cols = order_trig(jnp.int32(0), piece.shape[0])
    cos_add = jnp.dot(
        cos_cols,
        piece[:, 0, :],
        precision=lax.Precision.HIGHEST,
        preferred_element_type=jnp.float32,
    )
    sin_add = jnp.dot(
        sin_cols,
        piece[:, 1, :],
        precision=lax.Precision.HIGHEST,
        preferred_element_type=jnp.float32,
    )
    sal_field = cos_add + sin_add
    mixed = jnp.stack([surface - sal_field, water_depth, wet_cells, east_speed, north_speed])
    mixed_ext = with_halo(mixed, (("gy", 2), ("gx", 1)), 1)
    mixed_top = lax.all_gather(mixed[:3, :, -1], "gx", axis=1, tiled=True)
    mixed_ext = with_north(
        mixed_ext, partner_rows(mixed_top, fold_partner, lon_index, tile_lon), is_top
    )
    pressure_ext = mixed_ext[0]
    depth_ext = mixed_ext[1]
    wet_ext = mixed_ext[2]
    east_ext = mixed_ext[3]
    north_ext = mixed_ext[4]
    east_faces = (
        wet_ext[:-1, 1:-1]
        * wet_ext[1:, 1:-1]
        * (east_ext[:-1, 1:-1] - COURANT * (pressure_ext[1:, 1:-1] - pressure_ext[:-1, 1:-1]))
    )
    north_faces = (
        wet_ext[1:-1, :-1]
        * wet_ext[1:-1, 1:]
        * (north_ext[1:-1, :-1] - COURANT * (pressure_ext[1:-1, 1:] - pressure_ext[1:-1, :-1]))
    )
    east_flux = 0.5 * (depth_ext[:-1, 1:-1] + depth_ext[1:, 1:-1]) * east_faces
    north_flux = 0.5 * (depth_ext[1:-1, :-1] + depth_ext[1:-1, 1:]) * north_faces
    bottom_gate = jnp.where(lat_index > 0, 1.0, 0.0).astype(jnp.float32)
    south_flux = jnp.concatenate([north_flux[:, :1] * bottom_gate, north_flux[:, 1:-1]], axis=1)
    height_next = wet_cells * (
        surface - COURANT * (east_flux[1:] - east_flux[:-1] + north_flux[:, 1:] - south_flux)
    )
    return (sal_field, east_faces[1:], north_faces[:, 1:], height_next)


def solution(mesh):
    in_specs = (P("gx", "gy"), P("gx", "gy"), P("gx", "gy"), P("gx", "gy"), P("gx", "gy"), P(), P())
    out_specs = (P("gx", "gy"), P("gx", "gy"), P("gx", "gy"), P("gx", "gy"))
    return jax.shard_map(
        on_device, mesh=mesh, in_specs=in_specs, out_specs=out_specs, check_vma=False
    )
```

profile of v0, /device:TPU:0, one launch (start us, length us, event | category | flops | bytes accessed | tf_op | source)
XLA Modules:
  0.0 867.2 jit_solution(15962236669647059883)
XLA Ops:
  7.2 1.6 convolution_bitcast_fusion
  8.8 1.6 convolution_bitcast_fusion.1
  10.4 0.8 pad_maximum_fusion
  12.4 743.4 %while.21 = (s32[]{:T(128)}, f32[512,12]{0,1:T(8,128)S(1)}, f32[512,12]{0,1:T(8,128)S(1)}, f32[360,512,12]{1,2,0:T(8,128)}, s32[360]{0:T(512)S(1)}, /*index=5*/s...) while((s32[]{:T(128)}, f32[512,12]{0,1:T(8,128)S(1)}, ...), condition=%wide.region_5.6_spmd.clone.clone.clone, body=%wide.region_4.5_spmd.clone.clone.clone.sunk | while | flops 88395 | bytes 138387 | solution.py:137
  585.7 0.7 bitcast_dynamic-update-slice_fusion.4
  755.7 11.7 %broadcast_multiply_fusion = f32[360,512,12]{1,2,0:T(8,128)} fusion(f32[360,512,12]{1,2,0:T(8,128)} %get-tuple-element.151, f32[512,12]{0,1:T(8,128)S(1)} %negate_exponential_fusion), kind=kLoop, calls=%fused_computation.33 | loop fusion | flops 2211840 | bytes 17719296 | tf_op jit(solution)/shard_map/mul | solution.py:140
  767.5 1.5 copy.39
  768.9 6.4 all-to-all-start
  775.3 5.7 all-to-all-done
  781.0 15.9 %fusion.22 = f32[2,360,12]{1,0,2:T(2,128)S(1)} fusion(f32[360,512,12]{1,2,0:T(8,128)} %broadcast_multiply_fusion, f32[4,12,1,2,128]{4,3,2,1,0:T(2,128)S(1)} %bitcast.72, f32[512]{0:T(512)S(1)} %fusion.84, f32[12]{0:T(128)S(1)} %compare_select_fusion.8, f32[360]{0:T(512)S(1)} %copy-done.6), kind=kOutput, calls=%fused_computation.38 | convolution fusion | flops 53113728 | bytes 8934608 | tf_op jit(solution)/shard_map/ljs,scj->cls/dot_general | solution.py:142
  796.9 13.4 %fusion.12 = f32[12,2,512]{2,1,0:T(2,128)S(1)} fusion(f32[2,360,12]{1,0,2:T(2,128)S(1)} %fusion.22, f32[360,512,12]{1,2,0:T(8,128)} %broadcast_multiply_fusion), kind=kOutput, calls=%fused_computation.29 | convolution fusion | flops 53084160 | bytes 8931072 | tf_op jit(solution)/shard_map/cls,ljs->scj/dot_general | solution.py:147
  810.6 1.4 reshape.356
  812.1 3.3 all-to-all-start.1
  816.6 4.4 all-to-all-done.1
  821.5 0.8 reduce.8
  822.3 0.8 reshape.357
  823.3 9.6 %all_gather.6 = f32[384,2,128]{2,1,0:T(2,128)S(1)} all-gather(f32[48,2,128]{2,1,0:T(2,128)S(1)} %bitcast.73), channel_id=1, replica_groups=mesh['gy'=4,'gx'=8] {'gx'}, dimensions={0}, use_global_device_ids=true | all-gather | bytes 442368 | tf_op jit(solution)/shard_map/all_gather | solution.py:151
  834.6 0.7 collective-permute-start.1
  835.5 10.0 %all-gather = f32[3,384,1]{2,1,0:T(8,128)S(1)} all-gather(f32[3,48,1]{2,1,0:T(8,128)S(1)} %pad_maximum_fusion.2), channel_id=2, replica_groups=mesh['gy'=4,'gx'=8] {'gx'}, dimensions={1}, use_global_device_ids=true | all-gather | bytes 5184 | tf_op jit(solution)/shard_map/all_gather | solution.py:168
  845.4 1.3 collective-permute-start
  847.0 5.8 collective-permute-done
  853.0 2.6 collective-permute-start.3
  855.8 1.1 collective-permute-done.2
  857.1 0.9 scatter.4
  (1871 shorter events, 507.8 us)
Async XLA Ops:
  7.2 760.3 %reduce-scatter.2.cloned.1.call-start = ((), (), s32[]{:S(2)}) async-start(), calls=%async_computation.3 | async-start | bytes 442368 | tf_op jit(solution)/shard_map/reduce_scatter | solution.py:123
  755.7 25.3 %copy-start.6 = (f32[360]{0:T(512)S(1)}, f32[360]{0:T(512)}, u32[]{:S(2)}) copy-start(f32[360]{0:T(512)} %param.17) | copy-start | bytes 4324
  767.4 47.9 %copy-start = (s32[48,128]{1,0:T(8,128)S(1)}, s32[48,128]{1,0:T(8,128)}, u32[]{:S(2)}) copy-start(s32[48,128]{1,0:T(8,128)} %param.15) | copy-start | bytes 73732
  767.4 47.9 %copy-start.7 = (s32[8]{0:T(128)S(1)}, s32[8]{0:T(128)}, u32[]{:S(2)}) copy-start(s32[8]{0:T(128)} %param.16) | copy-start | bytes 100
  767.4 67.0 %copy-start.1 = (f32[48,128]{1,0:T(8,128)S(1)}, f32[48,128]{1,0:T(8,128)}, u32[]{:S(2)}) copy-start(f32[48,128]{1,0:T(8,128)} %param.11) | copy-start | bytes 73732
  767.4 67.0 %copy-start.2 = (f32[48,128]{1,0:T(8,128)S(1)}, f32[48,128]{1,0:T(8,128)}, u32[]{:S(2)}) copy-start(f32[48,128]{1,0:T(8,128)} %param.14) | copy-start | bytes 73732
  767.4 67.1 %copy-start.4 = (f32[48,128]{1,0:T(8,128)S(1)}, f32[48,128]{1,0:T(8,128)}, u32[]{:S(2)}) copy-start(f32[48,128]{1,0:T(8,128)} %param.12) | copy-start | bytes 73732
  767.4 67.1 %copy-start.5 = (f32[48,128]{1,0:T(8,128)S(1)}, f32[48,128]{1,0:T(8,128)}, u32[]{:S(2)}) copy-start(f32[48,128]{1,0:T(8,128)} %param.13) | copy-start | bytes 73732
  768.9 12.1 %all-to-all-start = ((f32[48,2,128]{2,1,0:T(2,128)}), f32[48,2,128]{2,1,0:T(2,128)S(1)}, u32[]{:S(2)}, u32[]{:S(2)}) async-start(f32[48,2,128]{2,1,0:T(2,128)} %copy.39), calls=%async_computation.1 | async-start | bytes 98304 | tf_op jit(solution)/shard_map/all_to_all | solution.py:126
  812.1 8.9 %all-to-all-start.1 = ((f32[4,1,3072]{2,1,0:T(1,128)}), f32[4,1,3072]{2,1,0:T(1,128)S(1)}, u32[]{:S(2)}, u32[]{:S(2)}) async-start(f32[4,1,3072]{2,1,0:T(1,128)} %reshape.356), calls=%async_computation.2 | async-start | bytes 98304 | tf_op jit(solution)/shard_map/all_to_all | solution.py:150
  834.4 26.0 %copy-start.3 = (f32[48,128]{1,0:T(8,128)}, f32[48,128]{1,0:T(8,128)S(1)}, u32[]{:S(2)}) copy-start(f32[48,128]{1,0:T(8,128)S(1)} %convolution_add_fusion) | copy-start | bytes 73732
  834.6 12.3 %collective-permute-start.1 = (f32[5,48,1]{2,1,0:T(8,128)S(1)}, f32[5,48,1]{2,1,0:T(8,128)S(1)}, u32[]{:S(2)}, u32[]{:S(2)}) collective-permute-start(f32[5,48,1]{2,1,0:T(8,128)S(1)} %get-tuple-element.288), channel_id=1, source_target_pairs={{8,0},{16,8},{24,16},{0,24},{9,1},{17,9},{25,17},{1,25},{10,2},{18... | collective-permute-start | bytes 2888 | tf_op jit(solution)/shard_map/ppermute | solution.py:19
  845.4 7.4 collective-permute-start
  852.9 4.0 collective-permute-start.2
  853.0 4.0 collective-permute-start.3
Sparse Core Ops, SparseCore 0:
  11.3 36.6 reduce-scatter.1
where the time goes:
time: 873 us; the launch traced here: 867 us
  other arithmetic  307 us (35%)
  loops' own time  243 us (28%)
  local copies, waits for them, and re-layouts  218 us (25%)
  matrix products  33.7 us (4%)
  blocking collectives  19.6 us (2%)
  waiting for transfers between devices  17.1 us (2%)
  between operations  15.1 us (2%)
  starting transfers between devices  14.4 us (2%)
    dynamic_update_slice x360, other arithmetic, on_device(): lax.scan(order_advance, (order_empty, order_empty), jnp.arange(degrees, d...  252 us
    another operation x1, loops' own time, on_device(): lax.scan(order_advance, (order_empty, order_empty), jnp.arange(degrees, d...  243 us
    dynamic_slice x360, local copies, waits for them, and re-layouts, on_device(): lax.scan(order_advance, (order_empty, order_empty), jnp.arange(degrees, d...  210 us
  transfers between devices with their start and end apart: 7, of which 4 were waited for; matrix products, arithmetic and copies ran while one was open for 59% of the time, Pallas kernels for 0%

commit v1 on v0

v1 whole, which is shorter than its diff:
```python
import math

import numpy as np

import jax
import jax.numpy as jnp
from jax import lax
from jax.experimental import pallas as pl
from jax.experimental.pallas import tpu as pltpu
from jax.sharding import PartitionSpec as P

COURANT = 0.35
GROUP = 8
STEPS = 32
ROWS = GROUP * STEPS
CHAINS = 2
EDGE = 8
F32 = jnp.float32
BF16 = jnp.bfloat16
HIGHEST = lax.Precision.HIGHEST


class Plan:
    def __init__(self, tile_lon, tile_lat, n_gx, n_gy, degrees):
        self.tile_lon, self.tile_lat = tile_lon, tile_lat
        self.n_gx, self.n_gy, self.degrees = n_gx, n_gy, degrees
        self.nlon, self.nlat = tile_lon * n_gx, tile_lat * n_gy
        self.half = self.nlat // 2
        self.n_groups = -(-degrees // GROUP)
        self.n_slots = -(-self.n_groups // n_gx)
        self.k_dev = 2 * self.n_slots * GROUP
        self.k_all = self.k_dev * n_gx
        self.group_of = np.array(
            [
                [s * n_gx + (c if s % 2 == 0 else n_gx - 1 - c) for s in range(self.n_slots)]
                for c in range(n_gx)
            ],
            np.int32,
        )
        self._schedule()
        self._tables()

    def _schedule(self):
        per_device = []
        for c in range(self.n_gx):
            work = []
            for s in range(self.n_slots):
                left = self.degrees - GROUP * int(self.group_of[c, s])
                if left > 0:
                    work.append((-(-left // STEPS), s))
            work.sort(reverse=True)
            chains = [[] for _ in range(CHAINS)]
            for chunks, s in work:
                chain = min(chains, key=len)
                chain.extend((s, k) for k in range(chunks))
            per_device.append(chains)
        longest = max(len(chain) for chains in per_device for chain in chains)
        self.n_iter = longest + longest % 2
        length = self.n_iter + 1
        table = np.zeros((self.n_gx, length, CHAINS, 2), np.int32)
        window = 0
        for c, chains in enumerate(per_device):
            for h, chain in enumerate(chains):
                filled = list(chain)
                while len(filled) < length:
                    s, k = filled[-1] if filled else (0, 0)
                    idle = -(-self.degrees // STEPS)
                    filled.append((s, max(k + 1, idle)))
                for i, (s, k) in enumerate(filled):
                    table[c, i, h] = (s, k)
                    window = max(window, int(self.group_of[c, s]) + k * (STEPS // GROUP))
        self.sched = table.reshape(-1)
        self.sched_stride = length * CHAINS * 2
        self.n_windows = -(-(window + 1) // 8) * 8
        self.love_rows = self.n_windows + 8

    def _tables(self):
        rows = np.arange(self.half)
        theta = np.pi * (rows + 0.5) / self.nlat
        self.geo = np.zeros((8, self.half), np.float32)
        self.geo[0] = np.cos(theta)
        self.geo[1] = np.log(np.sin(theta))
        all_theta = np.pi * (np.arange(self.nlat) + 0.5) / self.nlat
        quad = np.pi / self.nlat * (2.0 * np.pi / self.nlon) * np.sin(all_theta)
        self.quad = np.repeat(
            quad.reshape(self.n_gy, 1, self.tile_lat), 8, axis=1
        ).astype(np.float32)
        top = GROUP * (int(self.group_of.max()) + 1)
        factors = np.arange(1, top, dtype=np.float64)
        logs = np.concatenate([[0.0], np.cumsum(0.5 * np.log((2 * factors + 1) / (2 * factors)))])
        orders = self.group_of[:, :, None] * GROUP + np.arange(GROUP)[None, None, :]
        self.seed_logs = np.repeat(
            logs[orders].reshape(self.n_gx, self.n_slots * GROUP, 1), 128, axis=2
        ).astype(np.float32)
        lam = 2.0 * np.pi / self.nlon
        cols = np.arange(self.nlon)
        base = (self.group_of[:, :, None] * GROUP * cols[None, None, :]) % self.nlon
        u = np.stack([np.cos(lam * base), np.sin(lam * base)], axis=2)
        pad = -(-2 * self.n_slots // 8) * 8
        self.u_rows = pad
        self.u_table = np.zeros((self.n_gx, pad, self.nlon), np.float32)
        self.u_table[:, : 2 * self.n_slots] = u.reshape(self.n_gx, 2 * self.n_slots, self.nlon)
        small = (np.arange(GROUP)[:, None] * cols[None, :]) % self.nlon
        self.v_table = np.concatenate([np.cos(lam * small), np.sin(lam * small)]).astype(np.float32)
        m = np.concatenate(
            [np.tile(orders[c].reshape(-1), 2) for c in range(self.n_gx)]
        )
        sine = np.tile(np.repeat([0, 1], self.k_dev // 2), self.n_gx)
        nu = np.where(m == 0, 1.0, 2.0) * (m < self.degrees)
        starts = np.arange(self.n_gx) * self.tile_lon
        phase = lam * ((starts[:, None] * m[None, :]) % self.nlon)
        a1 = nu * np.where(sine == 0, np.cos(phase), np.sin(phase))
        a2 = nu * np.where(sine == 0, -np.sin(phase), np.cos(phase))
        self.a_table = np.zeros((self.n_gx, 8, self.k_all), np.float32)
        self.a_table[:, 0] = a1
        self.a_table[:, 1] = a2
        offsets = np.concatenate(
            [
                np.arange(self.tile_lon),
                [self.tile_lon, -1],
                np.zeros(EDGE - 2),
                np.arange(self.tile_lon)[::-1],
            ]
        ).astype(np.int64)
        phase = lam * ((offsets[:, None] * m[None, :]) % self.nlon)
        self.b_table = np.stack([np.cos(phase), np.sin(phase)]).astype(np.float32)
        self.o_rows = offsets.shape[0]


def iota(shape, axis):
    return lax.broadcasted_iota(jnp.int32, shape, axis)


def dot(a, b):
    return lax.dot_general(
        a, b, (((1,), (0,)), ((), ())), precision=HIGHEST, preferred_element_type=F32
    )


def flip_matrix(size, flipped):
    row = iota((size, size), 0)
    col = iota((size, size), 1)
    target = jnp.where(flipped, size - 1 - col, col)
    return jnp.where(row == target, 1.0, 0.0).astype(F32)


def pack_kernel(height, mask, depth, east, out, surface_out):
    lon, lat = height.shape
    wet = mask[...].astype(F32)
    surface = wet * height[...]
    surface_out[...] = surface
    out[:lon, :] = surface
    out[lon : lon + 1, :] = depth[:1, :]
    out[lon + 1 : lon + 2, :] = wet[:1, :]
    out[lon + 2 : lon + 3, :] = depth[lon - 1 :, :]
    out[lon + 3 : lon + 4, :] = wet[lon - 1 :, :]
    out[lon + 4 : lon + 5, :] = east[lon - 1 :, :]
    out[lon + 5 : lon + EDGE, :] = jnp.zeros((EDGE - 5, lat), F32)
    lane = iota((lon, lat), 1)
    out[lon + EDGE :, :] = jnp.where(
        lane == 0, depth[:, lat - 1 :], jnp.where(lane == 1, wet[:, lat - 1 :], 0.0)
    )


def fourier_kernel(plan, idx, fold, gathered, u, v, quad, surface, depth, mask, north, out, edges):
    lon, lat = plan.tile_lon, plan.tile_lat
    n_gx, slots = plan.n_gx, plan.n_slots
    c, r = idx[0], idx[1]
    field = jnp.concatenate([gathered[d, :lon, :] for d in range(n_gx)], axis=0)
    vc, vs = v[:GROUP, :], v[GROUP:, :]
    cos_rows, sin_rows = [], []
    for s in range(slots):
        uc = u[0, 2 * s : 2 * s + 1, :]
        us = u[0, 2 * s + 1 : 2 * s + 2, :]
        cos_rows.append(uc * vc - us * vs)
        sin_rows.append(us * vc + uc * vs)
    trig = jnp.concatenate(cos_rows + sin_rows, axis=0)
    sums = dot(trig, field) * quad[0, :1, :]
    out[lon:, :] = dot(sums, flip_matrix(lat, r >= plan.n_gy // 2))
    wet = mask[...].astype(F32)
    lane = iota((lon, lat), 1)
    tile = jnp.zeros((lon, lat), F32)
    last = [surface, depth, wet, north]
    for k, array in enumerate(last):
        tile = jnp.where(lane == k, array[:, lat - 1 :], tile)
    for k, array in enumerate([surface, depth, wet]):
        tile = jnp.where(lane == 4 + k, array[:, :1], tile)
    out[:lon, :] = tile
    after = lax.rem(c + 1, n_gx)
    before = lax.rem(c + n_gx - 1, n_gx)
    partner = fold[c]
    edges[0:1, :] = gathered[after, 0:1, :]
    edges[1:3, :] = gathered[after, lon : lon + 2, :]
    edges[3:4, :] = gathered[before, lon - 1 : lon, :]
    edges[4:7, :] = gathered[before, lon + 2 : lon + 5, :]
    edges[7:8, :] = jnp.zeros((1, lat), F32)
    across = jnp.where(
        lane == 2, gathered[partner, :lon, lat - 1 :], gathered[partner, lon + EDGE :, :]
    )
    edges[EDGE:, :] = dot(flip_matrix(lon, True), across)


def legendre_kernel(plan, idx, sched, *refs):
    n_gy, slots, half = plan.n_gy, plan.n_slots, plan.half
    lon, lat, k_half = plan.tile_lon, plan.tile_lat, plan.k_dev // 2
    blocks = refs[:n_gy]
    geo, seed_logs, love, out = refs[n_gy : n_gy + 4]
    (fabs, lhs, seeds, unscale, windows, acc, state, p_hi0, p_lo0, p_hi1, p_lo1, north_b, south_b) = refs[
        n_gy + 4 :
    ]
    c, r = idx[0], idx[1]
    n_half = n_gy // 2
    for k in range(n_gy):
        fabs[lax.rem(r - k + n_gy, n_gy)] = blocks[k][lon:, :]
    sym, anti = [], []
    for b in range(n_half):
        north, south = fabs[b], fabs[n_gy - 1 - b]
        sym.append(north + south)
        anti.append(north - south)
    sym = jnp.concatenate(sym, axis=1)
    anti = jnp.concatenate(anti, axis=1)
    log_sin = geo[1:2, :]
    sub = iota((GROUP, half), 0)
    for s in range(slots):
        lo, hi = s * GROUP, (s + 1) * GROUP
        rows = jnp.concatenate(
            [sym[lo:hi], anti[lo:hi], sym[k_half + lo : k_half + hi], anti[k_half + lo : k_half + hi]],
            axis=0,
        )
        rows_hi = rows.astype(BF16)
        lhs[s, : 4 * GROUP, :] = rows_hi
        lhs[s, 4 * GROUP :, :] = (rows - rows_hi.astype(F32)).astype(BF16)
        group = s * plan.n_gx + (c if s % 2 == 0 else plan.n_gx - 1 - c)
        order = (sub + group * GROUP).astype(F32)
        logs = jnp.concatenate([seed_logs[0, lo:hi, :]] * (half // 128), axis=1)
        exponent = order * log_sin + logs
        shift = jnp.clip(-exponent - 80.0, 0.0, 80.0)
        seeds[s] = jnp.exp(exponent + shift) * (1.0 / math.sqrt(4.0 * math.pi))
        unscale[s] = jnp.exp(-shift)
    acc[...] = jnp.zeros(acc.shape, F32)
    state[...] = jnp.zeros(state.shape, F32)
    spread = jnp.zeros((plan.n_windows, ROWS), F32)
    per = STEPS // GROUP
    for q in range(per):
        lane_degree = iota((GROUP, ROWS), 1) // GROUP - q * GROUP
        select = jnp.where(lane_degree == iota((GROUP, ROWS), 0), 1.0, 0.0).astype(F32)
        spread = spread + dot(love[q : q + plan.n_windows, :], select)
    windows[...] = spread.reshape(plan.n_windows, 1, ROWS)
    x = jnp.broadcast_to(geo[0:1, :], (GROUP, half))
    row = iota((4 * GROUP, ROWS), 0)
    lane = iota((4 * GROUP, ROWS), 1)
    i_row, i_lane, t_lane = row % GROUP, lane % GROUP, lane // GROUP
    keep = jnp.where(
        (i_row == i_lane) & ((t_lane + i_row) % 2 == (row // GROUP) % 2), 1.0, 0.0
    ).astype(F32)
    sub_c = iota((GROUP, 128), 0)
    lane_c = iota((GROUP, 128), 1)
    base = c * plan.sched_stride

    def item(i, h):
        at = base + (i * CHAINS + h) * 2
        slot, chunk = sched[at], sched[at + 1]
        even = lax.rem(slot, 2) == 0
        group = slot * plan.n_gx + jnp.where(even, c, plan.n_gx - 1 - c)
        return slot, chunk, group

    def generate(i, h, p_hi, p_lo):
        slot, chunk, group = item(i, h)
        first = chunk == 0
        m0 = group * GROUP
        degree = (m0 + chunk * STEPS + lane_c).astype(F32)
        order = (m0 + sub_c).astype(F32)
        below = degree - 1.0
        growth = jnp.sqrt(
            jnp.maximum(4.0 * degree * degree - 1.0, 1.0)
            / jnp.maximum(degree * degree - order * order, 1.0)
        )
        damping = jnp.sqrt(
            jnp.maximum(below * below - order * order, 0.0)
            / jnp.maximum(4.0 * below * below - 1.0, 1.0)
        )
        fall = growth * damping
        started = jnp.where(first, 0.0, 1.0).astype(F32)
        previous = state[h, 0] * started
        before = state[h, 1] * started
        seed = seeds[slot] * (1.0 - started)
        scale = unscale[slot]
        pair = []
        for t in range(STEPS):
            a = jnp.broadcast_to(growth[:, t : t + 1], (GROUP, half))
            b = jnp.broadcast_to(fall[:, t : t + 1], (GROUP, half))
            value = (a * x) * previous - b * before
            if t < GROUP:
                value = value + jnp.where(sub == t, seed, 0.0)
            previous, before = value, previous
            pair.append(value * scale)
            if t % 2 == 1:
                both = jnp.concatenate(pair, axis=0)
                both_hi = both.astype(BF16)
                at = (t - 1) * GROUP
                p_hi[h, at : at + 2 * GROUP, :] = both_hi
                p_lo[h, at : at + 2 * GROUP, :] = (both - both_hi.astype(F32)).astype(BF16)
                pair = []
        state[h, 0] = previous
        state[h, 1] = before

    def transform(i, h, p_hi, p_lo):
        slot, chunk, group = item(i, h)
        nt = (((1,), (1,)), ((), ()))
        nn = (((1,), (0,)), ((), ()))
        hi, lo = p_hi[h], p_lo[h]
        left = lhs[slot]
        n = 4 * GROUP
        one = lax.dot_general(left, hi, nt, preferred_element_type=F32)
        two = lax.dot_general(left[:n], lo, nt, preferred_element_type=F32)
        coeff = (one[:n] + one[n:] + two) * keep * windows[group + chunk * per]
        coeff_hi = coeff.astype(BF16)
        coeff_lo = (coeff - coeff_hi.astype(F32)).astype(BF16)
        right = jnp.concatenate([coeff_hi, coeff_lo], axis=0)
        three = lax.dot_general(right, hi, nn, preferred_element_type=F32)
        four = lax.dot_general(coeff_hi, lo, nn, preferred_element_type=F32)
        acc[slot] += three[:n] + three[n:] + four

    for h in range(CHAINS):
        generate(0, h, p_hi0, p_lo0)

    def body(k, carry):
        for h in range(CHAINS):
            transform(2 * k, h, p_hi0, p_lo0)
        for h in range(CHAINS):
            generate(2 * k + 1, h, p_hi1, p_lo1)
        for h in range(CHAINS):
            transform(2 * k + 1, h, p_hi1, p_lo1)
        for h in range(CHAINS):
            generate(2 * k + 2, h, p_hi0, p_lo0)
        return carry

    lax.fori_loop(0, plan.n_iter // 2, body, 0)

    for s in range(slots):
        lo, hi = s * GROUP, (s + 1) * GROUP
        g = acc[s]
        for part in range(2):
            even = g[2 * part * GROUP : (2 * part + 1) * GROUP]
            odd = g[(2 * part + 1) * GROUP : (2 * part + 2) * GROUP]
            for b in range(n_half):
                lanes = slice(b * lat, (b + 1) * lat)
                where = slice(part * k_half + lo, part * k_half + hi)
                north_b[b, where, :] = even[:, lanes] + odd[:, lanes]
                south_b[b, where, :] = even[:, lanes] - odd[:, lanes]
    is_north = r < n_half
    mine = jnp.where(is_north, r, n_gy - 1 - r)
    own = jnp.where(is_north, north_b[mine], south_b[mine])
    out[:, :lat] = dot(own, flip_matrix(lat, jnp.logical_not(is_north)))
    up_n = jnp.minimum(r + 1, n_half - 1)
    up_s = jnp.clip(n_gy - 2 - r, 0, n_half - 1)
    up = jnp.where(r + 1 < n_half, north_b[up_n][:, :1], south_b[up_s][:, lat - 1 :])
    down_n = jnp.clip(r - 1, 0, n_half - 1)
    down_s = jnp.clip(n_gy - r, 0, n_half - 1)
    down = jnp.where(r - 1 < n_half, north_b[down_n][:, lat - 1 :], south_b[down_s][:, :1])
    lane_o = iota((plan.k_dev, lat), 1)
    out[:, lat:] = jnp.where(lane_o == 0, up, jnp.where(lane_o == 1, down, 0.0))


def finish_kernel(
    plan, idx, fold, terms, a_own, a_fold, b_table, north_tile, south_tile, edges,
    surface_ref, depth_ref, mask, east_ref, north_ref,
    sal_out, east_out, north_out, height_out,
):
    lon, lat = plan.tile_lon, plan.tile_lat
    r = idx[1]
    split = lon + EDGE
    own_trig = a_own[0, 0:1, :] * b_table[0, :split, :] + a_own[0, 1:2, :] * b_table[1, :split, :]
    fold_trig = a_fold[0, 0:1, :] * b_table[0, split:, :] + a_fold[0, 1:2, :] * b_table[1, split:, :]
    trig = jnp.concatenate([own_trig, fold_trig], axis=0)
    sal_all = dot(trig, terms[...])
    sal = sal_all[:lon, :lat]
    sal_out[...] = sal
    is_top = r == plan.n_gy - 1
    sal_n = jnp.where(is_top, sal_all[split:, lat - 1 : lat], sal_all[:lon, lat : lat + 1])
    sal_s = sal_all[:lon, lat + 1 : lat + 2]
    surface, depth = surface_ref[...], depth_ref[...]
    wet = mask[...].astype(F32)
    east, north = east_ref[...], north_ref[...]
    across = edges[EDGE:, :]
    surf_n = jnp.where(is_top, across[:, 2:3], north_tile[:, 4:5])
    depth_n = jnp.where(is_top, across[:, 0:1], north_tile[:, 5:6])
    wet_n = jnp.where(is_top, across[:, 1:2], north_tile[:, 6:7])
    pressure = surface - sal
    row = iota((lon, lat), 0)
    lane = iota((lon, lat), 1)

    def east_of(field, edge):
        return jnp.where(row == lon - 1, edge, pltpu.roll(field, lon - 1, 0))

    def north_of(field, edge):
        return jnp.where(lane == lat - 1, edge, pltpu.roll(field, lat - 1, 1))

    p_e = edges[0:1, :] - sal_all[lon : lon + 1, :lat]
    p_w = edges[3:4, :] - sal_all[lon + 1 : lon + 2, :lat]
    east_next = wet * east_of(wet, edges[2:3, :]) * (
        east - COURANT * (east_of(pressure, p_e) - pressure)
    )
    north_next = wet * north_of(wet, wet_n) * (
        north - COURANT * (north_of(pressure, surf_n - sal_n) - pressure)
    )
    east_out[...] = east_next
    north_out[...] = north_next
    east_flux = 0.5 * (depth + east_of(depth, edges[1:2, :])) * east_next
    north_flux = 0.5 * (depth + north_of(depth, depth_n)) * north_next
    west_face = edges[5:6, :] * wet[:1] * (edges[6:7, :] - COURANT * (pressure[:1] - p_w))
    west_edge = 0.5 * (edges[4:5, :] + depth[:1]) * west_face
    south_face = south_tile[:, 2:3] * wet[:, :1] * (
        south_tile[:, 3:4] - COURANT * (pressure[:, :1] - (south_tile[:, 0:1] - sal_s))
    )
    south_edge = 0.5 * (south_tile[:, 1:2] + depth[:, :1]) * south_face
    south_edge = jnp.where(r > 0, south_edge, 0.0)
    west_flux = jnp.where(row == 0, west_edge, pltpu.roll(east_flux, 1, 0))
    south_flux = jnp.where(lane == 0, south_edge, pltpu.roll(north_flux, 1, 1))
    height_out[...] = wet * (
        surface - COURANT * (east_flux - west_flux + north_flux - south_flux)
    )


def full(shape):
    return pl.BlockSpec(shape, lambda i, *_: (0,) * len(shape))


def on_device(height, east_speed, north_speed, water_depth, ocean_mask, fold_partner, love_factor):
    lon, lat = height.shape
    n_gx, n_gy = lax.axis_size("gx"), lax.axis_size("gy")
    plan = Plan(lon, lat, n_gx, n_gy, love_factor.shape[0])
    idx = jnp.stack([lax.axis_index("gx"), lax.axis_index("gy")]).astype(jnp.int32)
    tile = jax.ShapeDtypeStruct((lon, lat), F32)
    sent = 2 * lon + EDGE
    packed, surface = pl.pallas_call(
        pack_kernel, out_shape=(jax.ShapeDtypeStruct((sent, lat), F32), tile), name="pack"
    )(height, ocean_mask, water_depth, east_speed)
    gathered = lax.all_gather(packed, "gx", axis=0, tiled=False)
    rows = lon + plan.k_dev
    tile_spec = full((lon, lat))
    mine, edges = pl.pallas_call(
        lambda *refs: fourier_kernel(plan, *refs),
        grid_spec=pltpu.PrefetchScalarGridSpec(
            num_scalar_prefetch=2,
            grid=(1,),
            in_specs=[
                full((n_gx, sent, lat)),
                pl.BlockSpec((1, plan.u_rows, plan.nlon), lambda i, idx, fold: (idx[0], 0, 0)),
                full((2 * GROUP, plan.nlon)),
                pl.BlockSpec((1, 8, lat), lambda i, idx, fold: (idx[1], 0, 0)),
                tile_spec, tile_spec, tile_spec, tile_spec,
            ],
            out_specs=[full((rows, lat)), full((lon + EDGE, lat))],
        ),
        out_shape=(
            jax.ShapeDtypeStruct((rows, lat), F32),
            jax.ShapeDtypeStruct((lon + EDGE, lat), F32),
        ),
        name="fourier",
    )(
        idx, fold_partner, gathered, plan.u_table, plan.v_table, plan.quad,
        surface, water_depth, ocean_mask, north_speed,
    )
    blocks = [mine]
    for k in range(1, n_gy):
        ring = [(i, (i + k) % n_gy) for i in range(n_gy)]
        blocks.append(lax.ppermute(mine, "gy", ring))
    padded = jnp.zeros((plan.love_rows * GROUP,), F32).at[: plan.degrees].set(love_factor)
    love = padded.reshape(plan.love_rows, GROUP)
    slots, half = plan.n_slots, plan.half
    p_shape = pltpu.VMEM((CHAINS, ROWS, half), BF16)
    split_shape = pltpu.VMEM((n_gy // 2, plan.k_dev, lat), F32)
    terms = pl.pallas_call(
        lambda *refs: legendre_kernel(plan, *refs),
        grid_spec=pltpu.PrefetchScalarGridSpec(
            num_scalar_prefetch=2,
            grid=(1,),
            in_specs=[full((rows, lat))] * n_gy
            + [
                full((8, half)),
                pl.BlockSpec((1, slots * GROUP, 128), lambda i, idx, sched: (idx[0], 0, 0)),
                full((plan.love_rows, GROUP)),
            ],
            out_specs=full((plan.k_dev, 2 * lat)),
            scratch_shapes=[
                pltpu.VMEM((n_gy, plan.k_dev, lat), F32),
                pltpu.VMEM((slots, 8 * GROUP, half), BF16),
                pltpu.VMEM((slots, GROUP, half), F32),
                pltpu.VMEM((slots, GROUP, half), F32),
                pltpu.VMEM((plan.n_windows, 1, ROWS), F32),
                pltpu.VMEM((slots, 4 * GROUP, half), F32),
                pltpu.VMEM((CHAINS, 2, GROUP, half), F32),
                p_shape, p_shape, p_shape, p_shape,
                split_shape, split_shape,
            ],
        ),
        out_shape=jax.ShapeDtypeStruct((plan.k_dev, 2 * lat), F32),
        name="legendre",
    )(idx, jnp.asarray(plan.sched), *blocks, plan.geo, plan.seed_logs, love)
    everything = lax.all_gather(terms, "gx", axis=0, tiled=True)
    halo_spec = full((lon, lat))
    a_spec = (1, 8, plan.k_all)
    return pl.pallas_call(
        lambda *refs: finish_kernel(plan, *refs),
        grid_spec=pltpu.PrefetchScalarGridSpec(
            num_scalar_prefetch=2,
            grid=(1,),
            in_specs=[
                full((plan.k_all, 2 * lat)),
                pl.BlockSpec(a_spec, lambda i, idx, fold: (idx[0], 0, 0)),
                pl.BlockSpec(a_spec, lambda i, idx, fold: (fold[idx[0]], 0, 0)),
                full((2, plan.o_rows, plan.k_all)),
                halo_spec, halo_spec,
                full((lon + EDGE, lat)),
                tile_spec, tile_spec, tile_spec, tile_spec, tile_spec,
            ],
            out_specs=[tile_spec] * 4,
        ),
        out_shape=(tile,) * 4,
        name="finish",
    )(
        idx, fold_partner, everything, plan.a_table, plan.a_table, plan.b_table,
        blocks[n_gy - 1], blocks[1], edges,
        surface, water_depth, ocean_mask, east_speed, north_speed,
    )


def solution(mesh):
    spec = P("gx", "gy")
    return jax.shard_map(
        on_device,
        mesh=mesh,
        in_specs=(spec, spec, spec, spec, spec, P(), P()),
        out_specs=(spec,) * 4,
        check_vma=False,
    )
```

time: 873 us -> 63.4 us (0.07)
  other arithmetic: 307 us -> 0.66 us
  loops' own time: 243 us -> 0 us
  local copies, waits for them, and re-layouts: 218 us -> 1.96 us
  matrix products: 33.7 us -> 0 us
  Pallas kernels: 0 us -> 24.5 us
  between operations: 15.1 us -> 0.65 us
  waiting for transfers between devices: 17.1 us -> 6.17 us
  starting transfers between devices: 14.4 us -> 4.62 us
    dynamic_update_slice x360 -> x0, other arithmetic: 252 us -> none  [on_device(): lax.scan(order_advance, (order_empty, order_empty), jnp.arange(degrees, d...]
    another operation x1 -> x0, loops' own time: 243 us -> none  [on_device(): lax.scan(order_advance, (order_empty, order_empty), jnp.arange(degrees, d...]
    dynamic_slice x362 -> x0, local copies, waits for them, and re-layouts: 210 us -> none  [the longest x360 210 us: on_device(): lax.scan(order_advance, (order_empty, order_empty), jnp.arange(degrees, d...]
    dot_general x6 -> x0, matrix products: 33.7 us -> none  [the longest x1 15.9 us: on_device(): jnp.einsum('ljs,scj->cls', order_legendre, order_weighted, precision=lax....]
    pallas_call x0 -> x4, Pallas kernels: none -> 24.5 us  [the longest x1 16.3 us: on_device(): pl.pallas_call(lambda *refs: legendre_kernel(plan, *refs), grid_spec=pltp...]
    cos x360 -> x0, other arithmetic: 15.7 us -> none  [latitude_rows(): return (jnp.cos(colatitude), sines, quadrature)]
    sqrt x360 -> x0, other arithmetic: 13.6 us -> none  [legendre_next(): jnp.sqrt(jnp.maximum(below_value * below_value - orders * orders, 0.0) /...]
    mul x7 -> x0, other arithmetic: 12.7 us -> none  [the longest x1 11.7 us: on_device(): order_legendre = order_scaled_legendre * order_unscale[None]]
  transfers between devices with their start and end apart: 7 -> 3, of which waited for: 4 -> 2; matrix products, arithmetic and copies ran while one was open for 59% -> 1% of each run, Pallas kernels for 0% -> 0%
where the time goes in v1:
time: 63.4 us; the launch traced here: 62.9 us
  Pallas kernels  24.5 us (39%)
  blocking collectives  24.4 us (38%)
  waiting for transfers between devices  6.17 us (10%)
  starting transfers between devices  4.62 us (7%)
  local copies, waits for them, and re-layouts  1.96 us (3%)
  other arithmetic  0.66 us (1%)
  between operations  0.65 us (1%)
    pallas_call x1, Pallas kernels, on_device(): pl.pallas_call(lambda *refs: legendre_kernel(plan, *refs), grid_spec=pltp...  16.3 us
    all_gather x1, blocking collectives, on_device(): gathered = lax.all_gather(packed, 'gx', axis=0, tiled=False)  13 us
    all_gather x1, blocking collectives, on_device(): everything = lax.all_gather(terms, 'gx', axis=0, tiled=True)  11.4 us
    ppermute x3, waiting for transfers between devices, on_device(): blocks.append(lax.ppermute(mine, 'gy', ring))  6.17 us
    ppermute x3, starting transfers between devices, on_device(): blocks.append(lax.ppermute(mine, 'gy', ring))  4.62 us
    pallas_call x1, Pallas kernels, on_device(): pl.pallas_call(lambda *refs: finish_kernel(plan, *refs), grid_spec=pltpu....  3.65 us
    pallas_call x1, Pallas kernels, on_device(): pl.pallas_call(lambda *refs: fourier_kernel(plan, *refs), grid_spec=pltpu...  3.06 us
    pallas_call x1, Pallas kernels, on_device(): pl.pallas_call(pack_kernel, out_shape=(jax.ShapeDtypeStruct((sent, lat),...  1.49 us
  transfers between devices with their start and end apart: 3, of which 2 were waited for; matrix products, arithmetic and copies ran while one was open for 1% of the time, Pallas kernels for 0%

profile of v1, /device:TPU:0, one launch (start us, length us, event | category | flops | bytes accessed | tf_op | source)
XLA Modules:
  0.0 62.9 jit_solution(1865714292496775764)
XLA Ops:
  0.6 1.5 %pack.1 = (f32[104,128]{1,0:T(8,128)}, f32[48,128]{1,0:T(8,128)}) custom-call(f32[48,128]{1,0:T(8,128)} %height.1, s32[48,128]{1,0:T(8,128)} %refs_11_.1, f32[48,128]{1,0:T(8,128)} %refs_10_.1, f32[48,128]{1,0:T(8,128)} %refs_12_.1), custom_call_target="tpu_custom_call" | custom-call | tf_op jit(solution)/shard_map/pack/pallas_call | solution.py:436
  2.1 13.0 %all-gather = f32[832,128]{1,0:T(8,128)} all-gather(f32[104,128]{1,0:T(8,128)} %get-tuple-element.20), channel_id=2, replica_groups=mesh['gy'=4,'gx'=8] {'gx'}, dimensions={0}, use_global_device_ids=true | all-gather | bytes 479232 | tf_op jit(solution)/shard_map/all_gather | solution.py:439
  15.2 0.7 %pad_add_fusion.refs_0_ = s32[2]{0:T(128)} fusion(s32[1]{0:T(128)} %bitcast.1, s32[1]{0:T(128)} %bitcast), kind=kLoop, calls=%fused_computation | loop fusion | flops 2 | bytes 16 | tf_op jit(solution)/shard_map/stack | solution.py:433
  15.8 0.0 copy-start.3
  15.8 3.1 %fourier.1 = (f32[144,128]{1,0:T(8,128)}, f32[56,128]{1,0:T(8,128)}) custom-call(s32[2]{0:T(128)} %pad_add_fusion.refs_0_, s32[8]{0:T(128)} %refs_1_.4, f32[8,104,128]{2,1,0:T(8,128)} %bitcast.3, f32[8,16,384]{2,1,0:T(8,128)} %constant.49.clone.refs_3_, f32[16,384]{1,0:T(8,128)} %constant.50.clone.refs_4_, f32[4,8,128]{2,1,0:T(8,128)} %constant.51.clone.refs_5_, ...), custom_call_target="tpu_custom_call" | custom-call | tf_op jit(solution)/shard_map/fourier/pallas_call | solution.py:442
  18.9 3.6 %collective-permute-start.2 = (f32[144,128]{1,0:T(8,128)}, f32[144,128]{1,0:T(8,128)S(1)}, u32[]{:S(2)}, u32[]{:S(2)}) collective-permute-start(f32[144,128]{1,0:T(8,128)} %get-tuple-element.22.refs_2_), channel_id=1, source_target_pairs={{0,24},{8,0},{16,8},{24,16},{1,25},{9,1},{17,9},{25,17},{2,26},{10... | collective-permute-start | bytes 221192 | tf_op jit(solution)/shard_map/ppermute | solution.py:468
  22.5 0.0 collective-permute-start.1
  22.5 1.0 %collective-permute-start = (f32[144,128]{1,0:T(8,128)}, f32[144,128]{1,0:T(8,128)S(1)}, u32[]{:S(2)}, u32[]{:S(2)}) collective-permute-start(f32[144,128]{1,0:T(8,128)} %get-tuple-element.22.refs_2_), channel_id=1, source_target_pairs={{0,8},{8,16},{16,24},{24,0},{1,9},{9,17},{17,25},{25,1},{2,10},{10... | collective-permute-start | bytes 221192 | tf_op jit(solution)/shard_map/ppermute | solution.py:468
  23.5 0.0 copy-done.3
  23.5 0.7 %reshape.33.refs_8_ = f32[120,8]{1,0:T(8,128)} reshape(f32[960]{0:T(1024)S(1)} %scatter.4) | data formatting | bytes 7680 | tf_op jit(solution)/shard_map/reshape | solution.py:470
  24.2 1.3 %collective-permute-done.2.refs_5_.refs_6_ = f32[144,128]{1,0:T(8,128)S(1)} collective-permute-done((f32[144,128]{1,0:T(8,128)}, f32[144,128]{1,0:T(8,128)S(1)}, u32[]{:S(2)}, u32[]{:S(2)}) %collective-permute-start.2) | collective-permute-done | bytes 73760 | tf_op jit(solution)/shard_map/ppermute | solution.py:468
  25.5 0.0 copy-start
  25.5 4.9 %collective-permute-done.1.refs_4_ = f32[144,128]{1,0:T(8,128)S(1)} collective-permute-done((f32[144,128]{1,0:T(8,128)}, f32[144,128]{1,0:T(8,128)S(1)}, u32[]{:S(2)}, u32[]{:S(2)}) %collective-permute-start.1) | collective-permute-done | bytes 73760 | tf_op jit(solution)/shard_map/ppermute | solution.py:468
  30.4 0.0 copy-start.2
  30.4 0.0 collective-permute-done.refs_3_.refs_7_
  30.4 0.0 copy-done
  30.4 0.6 copy-done.2
  31.0 0.0 copy-start.1
  31.0 0.6 copy-done.1
  31.6 16.3 %legendre.1 = f32[96,256]{1,0:T(8,128)} custom-call(s32[2]{0:T(128)} %pad_add_fusion.refs_0_, s32[672]{0:T(1024)} %constant.52.clone.refs_1_, f32[144,128]{1,0:T(8,128)} %get-tuple-element.22.refs_2_, f32[144,128]{1,0:T(8,128)} %copy-done.1, f32[144,128]{1,0:T(8,128)} %copy-done.2, f32[144,128]{1,0:T(8,128)} %copy-done, f32[8,256]{1,0:T(8,128)} %constant.53.clone.refs_6_, ...), custom_call_target="tpu_custom_call" | custom-call | tf_op jit(solution)/shard_map/legendre/pallas_call | solution.py:474
  47.9 11.4 %all_gather.11.refs_2_ = f32[768,256]{1,0:T(8,128)} all-gather(f32[96,256]{1,0:T(8,128)} %legendre.1), channel_id=1, replica_groups=mesh['gy'=4,'gx'=8] {'gx'}, dimensions={0}, use_global_device_ids=true | all-gather | bytes 884736 | tf_op jit(solution)/shard_map/all_gather | solution.py:501
  59.3 3.6 %finish.1 = (f32[48,128]{1,0:T(8,128)}, f32[48,128]{1,0:T(8,128)}, f32[48,128]{1,0:T(8,128)}, f32[48,128]{1,0:T(8,128)}) custom-call(s32[2]{0:T(128)} %pad_add_fusion.refs_0_, s32[8]{0:T(128)} %refs_1_.4, f32[768,256]{1,0:T(8,128)} %all_gather.11.refs_2_, f32[8,8,768]{2,1,0:T(8,128)} %constant.55.clone.refs_3_.refs_4_, ...), custom_call_target="tpu_custom_call" | custom-call | tf_op jit(solution)/shard_map/finish/pallas_call | solution.py:504
  (1 shorter events, 0.0 us)
Async XLA Ops:
  15.8 7.7 %copy-start.3 = (f32[360]{0:T(512)S(1)}, f32[360]{0:T(512)}, u32[]{:S(2)}) copy-start(f32[360]{0:T(512)} %param.23) | copy-start | bytes 4324
  18.9 6.6 %collective-permute-start.2 = (f32[144,128]{1,0:T(8,128)}, f32[144,128]{1,0:T(8,128)S(1)}, u32[]{:S(2)}, u32[]{:S(2)}) collective-permute-start(f32[144,128]{1,0:T(8,128)} %get-tuple-element.22.refs_2_), channel_id=1, source_target_pairs={{0,24},{8,0},{16,8},{24,16},{1,25},{9,1},{17,9},{25,17},{2,26},{10... | collective-permute-start | bytes 221192 | tf_op jit(solution)/shard_map/ppermute | solution.py:468
  22.5 7.9 %collective-permute-start.1 = (f32[144,128]{1,0:T(8,128)}, f32[144,128]{1,0:T(8,128)S(1)}, u32[]{:S(2)}, u32[]{:S(2)}) collective-permute-start(f32[144,128]{1,0:T(8,128)} %get-tuple-element.22.refs_2_), channel_id=1, source_target_pairs={{0,16},{8,24},{16,0},{24,8},{1,17},{9,25},{17,1},{25,9},{2,18},{10... | collective-permute-start | bytes 221192 | tf_op jit(solution)/shard_map/ppermute | solution.py:468
  22.5 7.9 %collective-permute-start = (f32[144,128]{1,0:T(8,128)}, f32[144,128]{1,0:T(8,128)S(1)}, u32[]{:S(2)}, u32[]{:S(2)}) collective-permute-start(f32[144,128]{1,0:T(8,128)} %get-tuple-element.22.refs_2_), channel_id=1, source_target_pairs={{0,8},{8,16},{16,24},{24,0},{1,9},{9,17},{17,25},{25,1},{2,10},{10... | collective-permute-start | bytes 221192 | tf_op jit(solution)/shard_map/ppermute | solution.py:468
  25.5 4.9 %copy-start = (f32[144,128]{1,0:T(8,128)}, f32[144,128]{1,0:T(8,128)S(1)}, u32[]{:S(2)}) copy-start(f32[144,128]{1,0:T(8,128)S(1)} %collective-permute-done.2.refs_5_.refs_6_) | copy-start | bytes 221188
  30.4 0.6 copy-start.2
  31.0 0.6 copy-start.1

commit v2 on v1

v2 whole, which is shorter than its diff:
```python
import math

import numpy as np

import jax
import jax.numpy as jnp
from jax import lax
from jax.experimental import pallas as pl
from jax.experimental.pallas import tpu as pltpu
from jax.sharding import PartitionSpec as P

COURANT = 0.35
GROUP = 8
STEPS = 32
ROWS = GROUP * STEPS
CHAINS = 2
UNROLL = 2
EDGE = 8
F32 = jnp.float32
BF16 = jnp.bfloat16
HIGHEST = lax.Precision.HIGHEST
PARAMS = pltpu.CompilerParams(vmem_limit_bytes=16 * 1024 * 1024)


class Plan:
    def __init__(self, tile_lon, tile_lat, n_gx, n_gy, degrees):
        self.tile_lon, self.tile_lat = tile_lon, tile_lat
        self.n_gx, self.n_gy, self.degrees = n_gx, n_gy, degrees
        self.nlon, self.nlat = tile_lon * n_gx, tile_lat * n_gy
        self.half = self.nlat // 2
        self.n_groups = -(-degrees // GROUP)
        self.n_slots = -(-self.n_groups // n_gx)
        self.k_dev = 2 * self.n_slots * GROUP
        self.k_all = self.k_dev * n_gx
        self.group_of = np.array(
            [
                [s * n_gx + (c if s % 2 == 0 else n_gx - 1 - c) for s in range(self.n_slots)]
                for c in range(n_gx)
            ],
            np.int32,
        )
        self._schedule()
        self._tables()

    def _schedule(self):
        lists = []
        for c in range(self.n_gx):
            counts = []
            for s in range(self.n_slots):
                left = self.degrees - GROUP * int(self.group_of[c, s])
                counts.append(-(-max(left, 0) // STEPS))
            lists.append(counts)
        longest = max(-(-sum(counts) // CHAINS) for counts in lists)
        longest = max(longest, max(max(counts) for counts in lists))
        self.n_iter = -(-longest // UNROLL) * UNROLL
        idle = -(-self.degrees // STEPS)
        per_row = self.n_iter * CHAINS * 2
        self.sched_width = -(-per_row // 128) * 128
        self.sched = np.zeros((self.n_gx, 1, self.sched_width), np.int32)
        for c, counts in enumerate(lists):
            first, second, room = [], [], self.n_iter
            for s, count in enumerate(counts):
                if room >= count:
                    first += [(s, k) for k in range(count)]
                    room -= count
                else:
                    head = count - room
                    second += [(s, k) for k in range(head)]
                    first += [(s, k) for k in range(head, count)]
                    room = 0
            last = max(range(self.n_slots), key=lambda s: counts[s])
            for chain in (first, second):
                while len(chain) < self.n_iter:
                    chain.append((self.n_slots, idle))
            for i in range(self.n_iter):
                for h, chain in enumerate((first, second)):
                    at = (i * CHAINS + h) * 2
                    self.sched[c, 0, at : at + 2] = chain[i]
        self.love_width = -(-(self.degrees + GROUP * self.n_gx * (self.n_slots + 1) + STEPS * (idle + 1)) // 128) * 128

    def _tables(self):
        rows = np.arange(self.half)
        theta = np.pi * (rows + 0.5) / self.nlat
        self.geo = np.zeros((8, self.half), np.float32)
        self.geo[0] = np.cos(theta)
        self.geo[1] = np.log(np.sin(theta))
        all_theta = np.pi * (np.arange(self.nlat) + 0.5) / self.nlat
        quad = np.pi / self.nlat * (2.0 * np.pi / self.nlon) * np.sin(all_theta)
        self.quad = np.repeat(
            quad.reshape(self.n_gy, 1, self.tile_lat), 8, axis=1
        ).astype(np.float32)
        top = GROUP * (int(self.group_of.max()) + 1)
        factors = np.arange(1, top, dtype=np.float64)
        logs = np.concatenate([[0.0], np.cumsum(0.5 * np.log((2 * factors + 1) / (2 * factors)))])
        orders = self.group_of[:, :, None] * GROUP + np.arange(GROUP)[None, None, :]
        lanes = -(-self.n_gx // 128) * 128
        self.seed_logs = np.zeros((self.n_slots * GROUP, lanes), np.float32)
        self.seed_logs[:, : self.n_gx] = logs[orders].reshape(self.n_gx, -1).T
        lam = 2.0 * np.pi / self.nlon
        cols = np.arange(self.nlon)
        base = (self.group_of[:, :, None] * GROUP * cols[None, None, :]) % self.nlon
        u = np.stack([np.cos(lam * base), np.sin(lam * base)], axis=2)
        pad = -(-2 * self.n_slots // 8) * 8
        self.u_rows = pad
        self.u_table = np.zeros((self.n_gx, pad, self.nlon), np.float32)
        self.u_table[:, : 2 * self.n_slots] = u.reshape(self.n_gx, 2 * self.n_slots, self.nlon)
        small = (np.arange(GROUP)[:, None] * cols[None, :]) % self.nlon
        self.v_table = np.concatenate([np.cos(lam * small), np.sin(lam * small)]).astype(np.float32)
        m = np.concatenate(
            [np.tile(orders[c].reshape(-1), 2) for c in range(self.n_gx)]
        )
        sine = np.tile(np.repeat([0, 1], self.k_dev // 2), self.n_gx)
        nu = np.where(m == 0, 1.0, 2.0) * (m < self.degrees)
        starts = np.arange(self.n_gx) * self.tile_lon
        phase = lam * ((starts[:, None] * m[None, :]) % self.nlon)
        a1 = nu * np.where(sine == 0, np.cos(phase), np.sin(phase))
        a2 = nu * np.where(sine == 0, -np.sin(phase), np.cos(phase))
        self.a_table = np.zeros((self.n_gx, 8, self.k_all), np.float32)
        self.a_table[:, 0] = a1
        self.a_table[:, 1] = a2
        offsets = np.concatenate(
            [
                np.arange(self.tile_lon),
                [self.tile_lon, -1],
                np.zeros(EDGE - 2),
                np.arange(self.tile_lon)[::-1],
            ]
        ).astype(np.int64)
        phase = lam * ((offsets[:, None] * m[None, :]) % self.nlon)
        self.b_table = np.stack([np.cos(phase), np.sin(phase)]).astype(np.float32)
        self.o_rows = offsets.shape[0]


def iota(shape, axis):
    return lax.broadcasted_iota(jnp.int32, shape, axis)


def dot(a, b):
    return lax.dot_general(
        a, b, (((1,), (0,)), ((), ())), precision=HIGHEST, preferred_element_type=F32
    )


def flip_matrix(size, flipped):
    row = iota((size, size), 0)
    col = iota((size, size), 1)
    target = jnp.where(flipped, size - 1 - col, col)
    return jnp.where(row == target, 1.0, 0.0).astype(F32)


def here():
    return lax.axis_index("gx"), lax.axis_index("gy")


def pack_kernel(plan, *refs):
    count = len(refs) // 2 - 1
    height, mask, depth, east = refs[:4]
    sources = refs[:count]
    out, surface_out = refs[count : count + 2]
    kept = refs[count + 2 : 2 * count + 1]
    height_v, sem = refs[2 * count + 1 :]
    c, r = here()
    targets = (height_v,) + tuple(kept)
    copies = []
    for k, (source, target) in enumerate(zip(sources, targets)):
        if k in SLICED_GX:
            source = source.at[c]
        elif k in SLICED_GY:
            source = source.at[r]
        copies.append(pltpu.make_async_copy(source, target, sem.at[k]))
    for copy in copies:
        copy.start()
    for copy in copies[:4]:
        copy.wait()
    _, mask_v, depth_v, east_v = targets[:4]
    lon, lat = height_v.shape
    wet = mask_v[...].astype(F32)
    surface = wet * height_v[...]
    surface_out[...] = surface
    out[:lon, :] = surface
    out[lon : lon + 1, :] = depth_v[:1, :]
    out[lon + 1 : lon + 2, :] = wet[:1, :]
    out[lon + 2 : lon + 3, :] = depth_v[lon - 1 :, :]
    out[lon + 3 : lon + 4, :] = wet[lon - 1 :, :]
    out[lon + 4 : lon + 5, :] = east_v[lon - 1 :, :]
    out[lon + 5 : lon + EDGE, :] = jnp.zeros((EDGE - 5, lat), F32)
    lane = iota((lon, lat), 1)
    out[lon + EDGE :, :] = jnp.where(
        lane == 0, depth_v[:, lat - 1 :], jnp.where(lane == 1, wet[:, lat - 1 :], 0.0)
    )
    for copy in copies[4:]:
        copy.wait()


def fourier_kernel(
    plan, gathered, u, v, quad, surface, depth, mask, north, fold_v, out, edges, fold, sem
):
    lon, lat = plan.tile_lon, plan.tile_lat
    n_gx, slots = plan.n_gx, plan.n_slots
    c, r = here()
    fetch = pltpu.make_async_copy(fold_v, fold, sem)
    fetch.start()
    field = jnp.concatenate([gathered[d, :lon, :] for d in range(n_gx)], axis=0)
    vc, vs = v[:GROUP, :], v[GROUP:, :]
    cos_rows, sin_rows = [], []
    for s in range(slots):
        uc = u[2 * s : 2 * s + 1, :]
        us = u[2 * s + 1 : 2 * s + 2, :]
        cos_rows.append(uc * vc - us * vs)
        sin_rows.append(us * vc + uc * vs)
    trig = jnp.concatenate(cos_rows + sin_rows, axis=0)
    sums = dot(trig, field) * quad[:1, :]
    out[lon:, :] = dot(sums, flip_matrix(lat, r >= plan.n_gy // 2))
    wet = mask[...].astype(F32)
    lane = iota((lon, lat), 1)
    tile = jnp.zeros((lon, lat), F32)
    last = [surface, depth, wet, north]
    for k, array in enumerate(last):
        tile = jnp.where(lane == k, array[:, lat - 1 :], tile)
    for k, array in enumerate([surface, depth, wet]):
        tile = jnp.where(lane == 4 + k, array[:, :1], tile)
    out[:lon, :] = tile
    after = lax.rem(c + 1, n_gx)
    before = lax.rem(c + n_gx - 1, n_gx)
    fetch.wait()
    partner = fold[c]
    edges[0:1, :] = gathered[after, 0:1, :]
    edges[1:3, :] = gathered[after, lon : lon + 2, :]
    edges[3:4, :] = gathered[before, lon - 1 : lon, :]
    edges[4:7, :] = gathered[before, lon + 2 : lon + 5, :]
    edges[7:8, :] = jnp.zeros((1, lat), F32)
    across = jnp.where(
        lane == 2, gathered[partner, :lon, lat - 1 :], gathered[partner, lon + EDGE :, :]
    )
    edges[EDGE:, :] = dot(flip_matrix(lon, True), across)


def scheduled(plan, c, sched, i, h):
    at = (i * CHAINS + h) * 2
    slot, chunk = sched[0, at], sched[0, at + 1]
    even = lax.rem(slot, 2) == 0
    group = slot * plan.n_gx + jnp.where(even, c, plan.n_gx - 1 - c)
    return slot, chunk, group


def basis_kernel(plan, sched_v, geo, seed_logs, p_out, seeds, unscale, state, sched, sem):
    slots, half = plan.n_slots, plan.half
    c, _ = here()
    fetch = pltpu.make_async_copy(sched_v, sched, sem)
    fetch.start()
    log_sin = geo[1:2, :]
    sub = iota((GROUP, half), 0)
    pick = iota(seed_logs.shape, 1) == c
    logs = jnp.sum(jnp.where(pick, seed_logs[...], 0.0), axis=1, keepdims=True)
    for s in range(slots):
        group = s * plan.n_gx + (c if s % 2 == 0 else plan.n_gx - 1 - c)
        order = (sub + group * GROUP).astype(F32)
        exponent = order * log_sin + logs[s * GROUP : (s + 1) * GROUP]
        shift = jnp.clip(-exponent - 80.0, 0.0, 80.0)
        seeds[s] = jnp.exp(exponent + shift) * (1.0 / math.sqrt(4.0 * math.pi))
        unscale[s] = jnp.exp(-shift)
    state[...] = jnp.zeros(state.shape, F32)
    seeds[slots] = jnp.zeros((GROUP, half), F32)
    unscale[slots] = jnp.zeros((GROUP, half), F32)
    x = jnp.broadcast_to(geo[0:1, :], (GROUP, half))
    sub_c = iota((GROUP, 128), 0)
    lane_c = iota((GROUP, 128), 1)
    fetch.wait()

    def begin(i, h):
        slot, chunk, group = scheduled(plan, c, sched, i, h)
        m0 = group * GROUP
        degree = (m0 + chunk * STEPS + lane_c).astype(F32)
        order = (m0 + sub_c).astype(F32)
        below = degree - 1.0
        growth = jnp.sqrt(
            jnp.maximum(4.0 * degree * degree - 1.0, 1.0)
            / jnp.maximum(degree * degree - order * order, 1.0)
        )
        damping = jnp.sqrt(
            jnp.maximum(below * below - order * order, 0.0)
            / jnp.maximum(4.0 * below * below - 1.0, 1.0)
        )
        started = jnp.where(chunk == 0, 0.0, 1.0).astype(F32)
        seed = seeds[slot] * (1.0 - started)
        return slot, growth, growth * damping, seed, unscale[slot], state[slot, 0], state[slot, 1]

    def body(i, carry):
        lanes = [begin(i, h) for h in range(CHAINS)]
        previous = [lane[5] for lane in lanes]
        before = [lane[6] for lane in lanes]
        pairs = [[] for _ in range(CHAINS)]
        for t in range(STEPS):
            for h, (_, growth, fall, seed, scale, _, _) in enumerate(lanes):
                a = jnp.broadcast_to(growth[:, t : t + 1], (GROUP, half))
                b = jnp.broadcast_to(fall[:, t : t + 1], (GROUP, half))
                value = (a * x) * previous[h] - b * before[h]
                if t < GROUP:
                    value = value + jnp.where(sub == t, seed, 0.0)
                previous[h], before[h] = value, previous[h]
                pairs[h].append(value * scale)
                if t % 2 == 1:
                    both = jnp.concatenate(pairs[h], axis=0)
                    both_hi = both.astype(BF16)
                    at = (t - 1) * GROUP
                    p_out[i, h, 0, at : at + 2 * GROUP, :] = both_hi
                    p_out[i, h, 1, at : at + 2 * GROUP, :] = (
                        both - both_hi.astype(F32)
                    ).astype(BF16)
                    pairs[h] = []
        for h, lane in enumerate(lanes):
            state[lane[0], 0] = previous[h]
            state[lane[0], 1] = before[h]
        return carry

    lax.fori_loop(0, plan.n_iter, body, 0)


def legendre_kernel(plan, *refs):
    n_gy, slots, half = plan.n_gy, plan.n_slots, plan.half
    lon, lat, k_half = plan.tile_lon, plan.tile_lat, plan.k_dev // 2
    blocks = refs[:n_gy]
    basis, love, sched_v, out = refs[n_gy : n_gy + 4]
    (fabs, lhs, weights, shifted, acc, coeffs, north_b, south_b, sched, sem) = refs[n_gy + 4 :]
    c, r = here()
    fetch = pltpu.make_async_copy(sched_v, sched, sem)
    fetch.start()
    n_half = n_gy // 2
    for k in range(n_gy):
        fabs[lax.rem(r - k + n_gy, n_gy)] = blocks[k][lon:, :]
    sym, anti = [], []
    for b in range(n_half):
        north, south = fabs[b], fabs[n_gy - 1 - b]
        sym.append(north + south)
        anti.append(north - south)
    sym = jnp.concatenate(sym, axis=1)
    anti = jnp.concatenate(anti, axis=1)
    for s in range(slots):
        lo, hi = s * GROUP, (s + 1) * GROUP
        rows = jnp.concatenate(
            [sym[lo:hi], anti[lo:hi], sym[k_half + lo : k_half + hi], anti[k_half + lo : k_half + hi]],
            axis=0,
        )
        rows_hi = rows.astype(BF16)
        lhs[s, : 4 * GROUP, :] = rows_hi
        lhs[s, 4 * GROUP :, :] = (rows - rows_hi.astype(F32)).astype(BF16)
    acc[...] = jnp.zeros(acc.shape, F32)
    lhs[slots] = jnp.zeros((8 * GROUP, half), BF16)
    padded = jnp.concatenate(
        [love[...].reshape(1, -1), jnp.zeros((1, plan.love_width - plan.degrees), F32)], axis=1
    )
    padded = jnp.broadcast_to(padded, (8, plan.love_width))
    fetch.wait()
    items = plan.n_iter * CHAINS
    for item in range(items):
        _, chunk, group = scheduled(plan, c, sched, item // CHAINS, item % CHAINS)
        start = group * GROUP + chunk * STEPS
        rolled = pltpu.roll(padded, plan.love_width - start, 1)
        shifted[item : item + 1, :] = rolled[:1, :128]
    spread = iota((128, ROWS), 1) // GROUP == iota((128, ROWS), 0)
    weights[...] = dot(shifted[...], jnp.where(spread, 1.0, 0.0).astype(F32)).reshape(
        items, 1, ROWS
    )
    row = iota((4 * GROUP, ROWS), 0)
    lane = iota((4 * GROUP, ROWS), 1)
    i_row, i_lane, t_lane = row % GROUP, lane % GROUP, lane // GROUP
    keep = jnp.where(
        (i_row == i_lane) & ((t_lane + i_row) % 2 == (row // GROUP) % 2), 1.0, 0.0
    ).astype(F32)
    nt = (((1,), (1,)), ((), ()))
    nn = (((1,), (0,)), ((), ()))
    n = 4 * GROUP

    def analyse(i, h):
        slot, _, _ = scheduled(plan, c, sched, i, h)
        left = lhs[slot]
        one = lax.dot_general(left, basis[i, h, 0], nt, preferred_element_type=F32)
        two = lax.dot_general(left[:n], basis[i, h, 1], nt, preferred_element_type=F32)
        coeff = (one[:n] + one[n:] + two) * keep * weights[i * CHAINS + h]
        coeff_hi = coeff.astype(BF16)
        coeff_lo = (coeff - coeff_hi.astype(F32)).astype(BF16)
        return jnp.concatenate([coeff_hi, coeff_lo], axis=0)

    def synthesise(i, h):
        right = coeffs[i, h]
        three = lax.dot_general(right, basis[i, h, 0], nn, preferred_element_type=F32)
        four = lax.dot_general(right[:n], basis[i, h, 1], nn, preferred_element_type=F32)
        return three[:n] + three[n:] + four

    def analyse_all(k):
        for j in range(UNROLL):
            for h in range(CHAINS):
                i = k * UNROLL + j
                coeffs[i, h] = analyse(i, h)

    def synthesise_all(k):
        found = [
            (scheduled(plan, c, sched, k * UNROLL + j, h)[0], synthesise(k * UNROLL + j, h))
            for j in range(UNROLL)
            for h in range(CHAINS)
        ]
        return found

    def accumulate(found):
        for slot, part in found:
            acc[slot] += part

    trips = plan.n_iter // UNROLL
    analyse_all(0)

    def body(k, carry):
        found = synthesise_all(k - 1)
        analyse_all(k)
        accumulate(found)
        return carry

    lax.fori_loop(1, trips, body, 0)
    accumulate(synthesise_all(trips - 1))

    for s in range(slots):
        lo, hi = s * GROUP, (s + 1) * GROUP
        g = acc[s]
        for part in range(2):
            even = g[2 * part * GROUP : (2 * part + 1) * GROUP]
            odd = g[(2 * part + 1) * GROUP : (2 * part + 2) * GROUP]
            for b in range(n_half):
                lanes = slice(b * lat, (b + 1) * lat)
                where = slice(part * k_half + lo, part * k_half + hi)
                north_b[b, where, :] = even[:, lanes] + odd[:, lanes]
                south_b[b, where, :] = even[:, lanes] - odd[:, lanes]
    is_north = r < n_half
    mine = jnp.where(is_north, r, n_gy - 1 - r)
    own = jnp.where(is_north, north_b[mine], south_b[mine])
    out[:, :lat] = dot(own, flip_matrix(lat, jnp.logical_not(is_north)))
    up_n = jnp.minimum(r + 1, n_half - 1)
    up_s = jnp.clip(n_gy - 2 - r, 0, n_half - 1)
    up = jnp.where(r + 1 < n_half, north_b[up_n][:, :1], south_b[up_s][:, lat - 1 :])
    down_n = jnp.clip(r - 1, 0, n_half - 1)
    down_s = jnp.clip(n_gy - r, 0, n_half - 1)
    down = jnp.where(r - 1 < n_half, north_b[down_n][:, lat - 1 :], south_b[down_s][:, :1])
    lane_o = iota((plan.k_dev, lat), 1)
    out[:, lat:] = jnp.where(lane_o == 0, up, jnp.where(lane_o == 1, down, 0.0))


def finish_kernel(
    plan, terms, a_table, b_table, fold_v, north_tile, south_tile, edges,
    surface_ref, depth_ref, mask, east_ref, north_ref,
    sal_out, east_out, north_out, height_out, fold, sem,
):
    lon, lat = plan.tile_lon, plan.tile_lat
    c, r = here()
    fetch = pltpu.make_async_copy(fold_v, fold, sem)
    fetch.start()
    split = lon + EDGE
    a_own = a_table[c]
    own_trig = a_own[0:1, :] * b_table[0, :split, :] + a_own[1:2, :] * b_table[1, :split, :]
    fetch.wait()
    a_fold = a_table[fold[c]]
    fold_trig = a_fold[0:1, :] * b_table[0, split:, :] + a_fold[1:2, :] * b_table[1, split:, :]
    trig = jnp.concatenate([own_trig, fold_trig], axis=0)
    sal_all = dot(trig, terms[...])
    sal = sal_all[:lon, :lat]
    sal_out[...] = sal
    is_top = r == plan.n_gy - 1
    sal_n = jnp.where(is_top, sal_all[split:, lat - 1 : lat], sal_all[:lon, lat : lat + 1])
    sal_s = sal_all[:lon, lat + 1 : lat + 2]
    surface, depth = surface_ref[...], depth_ref[...]
    wet = mask[...].astype(F32)
    east, north = east_ref[...], north_ref[...]
    across = edges[EDGE:, :]
    surf_n = jnp.where(is_top, across[:, 2:3], north_tile[:lon, 4:5])
    depth_n = jnp.where(is_top, across[:, 0:1], north_tile[:lon, 5:6])
    wet_n = jnp.where(is_top, across[:, 1:2], north_tile[:lon, 6:7])
    pressure = surface - sal
    row = iota((lon, lat), 0)
    lane = iota((lon, lat), 1)

    def east_of(field, edge):
        return jnp.where(row == lon - 1, edge, pltpu.roll(field, lon - 1, 0))

    def north_of(field, edge):
        return jnp.where(lane == lat - 1, edge, pltpu.roll(field, lat - 1, 1))

    p_e = edges[0:1, :] - sal_all[lon : lon + 1, :lat]
    p_w = edges[3:4, :] - sal_all[lon + 1 : lon + 2, :lat]
    east_next = wet * east_of(wet, edges[2:3, :]) * (
        east - COURANT * (east_of(pressure, p_e) - pressure)
    )
    north_next = wet * north_of(wet, wet_n) * (
        north - COURANT * (north_of(pressure, surf_n - sal_n) - pressure)
    )
    east_out[...] = east_next
    north_out[...] = north_next
    east_flux = 0.5 * (depth + east_of(depth, edges[1:2, :])) * east_next
    north_flux = 0.5 * (depth + north_of(depth, depth_n)) * north_next
    west_face = edges[5:6, :] * wet[:1] * (edges[6:7, :] - COURANT * (pressure[:1] - p_w))
    west_edge = 0.5 * (edges[4:5, :] + depth[:1]) * west_face
    south_face = south_tile[:lon, 2:3] * wet[:, :1] * (
        south_tile[:lon, 3:4] - COURANT * (pressure[:, :1] - (south_tile[:lon, 0:1] - sal_s))
    )
    south_edge = 0.5 * (south_tile[:lon, 1:2] + depth[:, :1]) * south_face
    south_edge = jnp.where(r > 0, south_edge, 0.0)
    west_flux = jnp.where(row == 0, west_edge, pltpu.roll(east_flux, 1, 0))
    south_flux = jnp.where(lane == 0, south_edge, pltpu.roll(north_flux, 1, 1))
    height_out[...] = wet * (
        surface - COURANT * (east_flux - west_flux + north_flux - south_flux)
    )


VMEM = pl.BlockSpec(memory_space=pltpu.VMEM)
HBM = pl.BlockSpec(memory_space=pltpu.HBM)
SLICED_GX = (5, 10)
SLICED_GY = (7,)


def on_device(height, east_speed, north_speed, water_depth, ocean_mask, fold_partner, love_factor):
    lon, lat = height.shape
    n_gx, n_gy = lax.axis_size("gx"), lax.axis_size("gy")
    plan = Plan(lon, lat, n_gx, n_gy, love_factor.shape[0])
    slots, half = plan.n_slots, plan.half
    sent = 2 * lon + EDGE
    sources = (
        height, ocean_mask, water_depth, east_speed, north_speed, plan.u_table, plan.v_table,
        plan.quad, plan.geo, plan.seed_logs, plan.sched, love_factor, fold_partner,
    )
    sources = tuple(
        pltpu.with_memory_space_constraint(jnp.asarray(source), pltpu.HBM) for source in sources
    )
    kept_shapes = [
        source.shape[1:] if k in SLICED_GX + SLICED_GY else source.shape
        for k, source in enumerate(sources)
    ]
    kept = [
        pltpu.VMEM(shape, source.dtype) for shape, source in zip(kept_shapes[1:], sources[1:])
    ]
    packed, surface, *kept = pl.pallas_call(
        lambda *refs: pack_kernel(plan, *refs),
        in_specs=[HBM] * len(sources),
        out_specs=[VMEM] * (len(sources) + 1),
        out_shape=(pltpu.VMEM((sent, lat), F32), pltpu.VMEM((lon, lat), F32), *kept),
        scratch_shapes=[pltpu.VMEM((lon, lat), F32), pltpu.SemaphoreType.DMA((len(sources),))],
        compiler_params=PARAMS,
        name="pack",
    )(*sources)
    mask, depth, east, north, u, v, quad, geo, seed_logs, sched, love, fold = kept
    gathered = lax.all_gather(packed, "gx", axis=0, tiled=False)
    rows = lon + plan.k_dev
    fold_scratch = [pltpu.SMEM((n_gx,), jnp.int32), pltpu.SemaphoreType.DMA]
    mine, edges = pl.pallas_call(
        lambda *refs: fourier_kernel(plan, *refs),
        in_specs=[VMEM] * 9,
        out_specs=[VMEM] * 2,
        out_shape=(pltpu.VMEM((rows, lat), F32), pltpu.VMEM((lon + EDGE, lat), F32)),
        scratch_shapes=fold_scratch,
        compiler_params=PARAMS,
        name="fourier",
    )(gathered, u, v, quad, surface, depth, mask, north, fold)
    blocks = [mine]
    for k in range(1, n_gy):
        ring = [(i, (i + k) % n_gy) for i in range(n_gy)]
        blocks.append(lax.ppermute(mine, "gy", ring))
    sched_scratch = [pltpu.SMEM((1, plan.sched_width), jnp.int32), pltpu.SemaphoreType.DMA]
    basis = pl.pallas_call(
        lambda *refs: basis_kernel(plan, *refs),
        in_specs=[VMEM] * 3,
        out_specs=VMEM,
        out_shape=pltpu.VMEM((plan.n_iter, CHAINS, 2, ROWS, half), BF16),
        scratch_shapes=[
            pltpu.VMEM((slots + 1, GROUP, half), F32),
            pltpu.VMEM((slots + 1, GROUP, half), F32),
            pltpu.VMEM((slots + 1, 2, GROUP, half), F32),
        ]
        + sched_scratch,
        cost_estimate=pl.CostEstimate(flops=60_000_000, bytes_accessed=1_000_000, transcendentals=0),
        compiler_params=PARAMS,
        name="basis",
    )(sched, geo, seed_logs)
    items = plan.n_iter * CHAINS
    split_shape = pltpu.VMEM((n_gy // 2, plan.k_dev, lat), F32)
    terms = pl.pallas_call(
        lambda *refs: legendre_kernel(plan, *refs),
        in_specs=[VMEM] * (n_gy + 3),
        out_specs=VMEM,
        out_shape=pltpu.VMEM((plan.k_dev, 2 * lat), F32),
        scratch_shapes=[
            pltpu.VMEM((n_gy, plan.k_dev, lat), F32),
            pltpu.VMEM((slots + 1, 8 * GROUP, half), BF16),
            pltpu.VMEM((items, 1, ROWS), F32),
            pltpu.VMEM((items, 128), F32),
            pltpu.VMEM((slots + 1, 4 * GROUP, half), F32),
            pltpu.VMEM((plan.n_iter, CHAINS, 8 * GROUP, ROWS), BF16),
            split_shape, split_shape,
        ]
        + sched_scratch,
        compiler_params=PARAMS,
        name="legendre",
    )(*blocks, basis, love, sched)
    everything = lax.all_gather(terms, "gx", axis=0, tiled=True)
    tile = jax.ShapeDtypeStruct((lon, lat), F32)
    a_table, b_table = jnp.asarray(plan.a_table), jnp.asarray(plan.b_table)
    return pl.pallas_call(
        lambda *refs: finish_kernel(plan, *refs),
        in_specs=[VMEM] * 12,
        out_specs=[VMEM] * 4,
        out_shape=(tile,) * 4,
        scratch_shapes=fold_scratch,
        compiler_params=PARAMS,
        name="finish",
    )(
        everything, a_table, b_table, fold, blocks[n_gy - 1], blocks[1], edges,
        surface, depth, mask, east, north,
    )


def solution(mesh):
    spec = P("gx", "gy")
    return jax.shard_map(
        on_device,
        mesh=mesh,
        in_specs=(spec, spec, spec, spec, spec, P(), P()),
        out_specs=(spec,) * 4,
        check_vma=False,
    )
```

time: 63.4 us -> 44.6 us (0.70)
  Pallas kernels: 24.5 us -> 16.6 us
  waiting for transfers between devices: 6.17 us -> 0.87 us
  blocking collectives: 24.4 us -> 21.6 us
  local copies, waits for them, and re-layouts: 1.96 us -> 0.01 us
  other arithmetic: 0.66 us -> 0 us
    pallas_call x4 -> x5, Pallas kernels: 24.5 us -> 16.6 us  [the longest x1 6.67 us: on_device(): pl.pallas_call(lambda *refs: legendre_kernel(plan, *refs), in_specs=[VMEM...]
    ppermute x3, waiting for transfers between devices: 6.17 us -> 0.87 us  [on_device(): blocks.append(lax.ppermute(mine, 'gy', ring))]
    all_gather x1, blocking collectives: 13 us -> 11.2 us  [on_device(): gathered = lax.all_gather(packed, 'gx', axis=0, tiled=False)]
    unnamed x8 -> x4, local copies, waits for them, and re-layouts: 1.24 us -> 0.01 us
    all_gather x1, blocking collectives: 11.4 us -> 10.4 us  [on_device(): everything = lax.all_gather(terms, 'gx', axis=0, tiled=True)]
    reshape x1 -> x0, local copies, waits for them, and re-layouts: 0.71 us -> none  [on_device(): love = padded.reshape(plan.love_rows, GROUP)]
    another operation x1 -> x0, other arithmetic: 0.66 us -> none  [on_device(): jnp.stack([lax.axis_index('gx'), lax.axis_index('gy')]).astype(jnp.int32)]
  transfers between devices with their start and end apart: 3 -> 3, of which waited for: 2 -> 1; matrix products, arithmetic and copies ran while one was open for 1% -> 0% of each run, Pallas kernels for 0% -> 13%
where the time goes in v2:
time: 44.6 us; the launch traced here: 44.4 us
  blocking collectives  21.6 us (48%)
  Pallas kernels  16.6 us (37%)
  starting transfers between devices  4.66 us (10%)
  waiting for transfers between devices  0.87 us (2%)
  between operations  0.68 us (2%)
    all_gather x1, blocking collectives, on_device(): gathered = lax.all_gather(packed, 'gx', axis=0, tiled=False)  11.2 us
    all_gather x1, blocking collectives, on_device(): everything = lax.all_gather(terms, 'gx', axis=0, tiled=True)  10.4 us
    pallas_call x1, Pallas kernels, on_device(): pl.pallas_call(lambda *refs: legendre_kernel(plan, *refs), in_specs=[VMEM...  6.67 us
    pallas_call x1, Pallas kernels, on_device(): pl.pallas_call(lambda *refs: basis_kernel(plan, *refs), in_specs=[VMEM] *...  5.79 us
    ppermute x3, starting transfers between devices, on_device(): blocks.append(lax.ppermute(mine, 'gy', ring))  4.66 us
    pallas_call x1, Pallas kernels, on_device(): pl.pallas_call(lambda *refs: finish_kernel(plan, *refs), in_specs=[VMEM]...  2.1 us
    pallas_call x1, Pallas kernels, on_device(): pl.pallas_call(lambda *refs: pack_kernel(plan, *refs), in_specs=[HBM] * l...  1.03 us
    pallas_call x1, Pallas kernels, on_device(): pl.pallas_call(lambda *refs: fourier_kernel(plan, *refs), in_specs=[VMEM]...  0.98 us
  transfers between devices with their start and end apart: 3, of which 1 were waited for; matrix products, arithmetic and copies ran while one was open for 0% of the time, Pallas kernels for 13%

profile of v2, /device:TPU:0, one launch (start us, length us, event | category | flops | bytes accessed | tf_op | source)
XLA Modules:
  0.0 44.4 jit_solution(14138840572437164515)
XLA Ops:
  0.6 1.0 %pack.1 = (f32[104,128]{1,0:T(8,128)S(1)}, f32[48,128]{1,0:T(8,128)S(1)}, s32[48,128]{1,0:T(8,128)S(1)}, f32[48,128]{1,0:T(8,128)S(1)}, f32[48,128]{1,0:T(8,128)...) custom-call(f32[48,128]{1,0:T(8,128)} %refs_0_.1, ...), custom_call_target="tpu_custom_call" | custom-call | tf_op jit(solution)/shard_map/pack/pallas_call | solution.py:536
  1.7 11.2 %all-gather = f32[832,128]{1,0:T(8,128)S(1)} all-gather(f32[104,128]{1,0:T(8,128)S(1)} %get-tuple-element.20), channel_id=2, replica_groups=mesh['gy'=4,'gx'=8] {'gx'}, dimensions={0}, use_global_device_ids=true | all-gather | bytes 479232 | tf_op jit(solution)/shard_map/all_gather | solution.py:546
  12.9 1.0 %fourier.1 = (f32[144,128]{1,0:T(8,128)S(1)}, f32[56,128]{1,0:T(8,128)S(1)}) custom-call(f32[8,104,128]{2,1,0:T(8,128)S(1)} %bitcast.1, f32[16,384]{1,0:T(8,128)S(1)} %get-tuple-element.21.refs_1_, f32[16,384]{1,0:T(8,128)S(1)} %get-tuple-element.22.refs_2_, f32[8,128]{1,0:T(8,128)S(1)} %get-tuple-element.23.refs_3_, ...), custom_call_target="tpu_custom_call" | custom-call | tf_op jit(solution)/shard_map/fourier/pallas_call | solution.py:549
  13.9 3.7 %collective-permute-start.2 = (f32[144,128]{1,0:T(8,128)S(1)}, f32[144,128]{1,0:T(8,128)S(1)}, u32[]{:S(2)}, u32[]{:S(2)}) collective-permute-start(f32[144,128]{1,0:T(8,128)S(1)} %get-tuple-element.29.refs_0_), channel_id=1, source_target_pairs={{0,24},{8,0},{16,8},{24,16},{1,25},{9,1},{17,9},{25,17},{2,26},{10... | collective-permute-start | bytes 221192 | tf_op jit(solution)/shard_map/ppermute | solution.py:561
  17.5 0.0 collective-permute-start.1
  17.5 1.0 %collective-permute-start = (f32[144,128]{1,0:T(8,128)S(1)}, f32[144,128]{1,0:T(8,128)S(1)}, u32[]{:S(2)}, u32[]{:S(2)}) collective-permute-start(f32[144,128]{1,0:T(8,128)S(1)} %get-tuple-element.29.refs_0_), channel_id=1, source_target_pairs={{0,8},{8,16},{16,24},{24,0},{1,9},{9,17},{17,25},{25,1},{2,10},{10... | collective-permute-start | bytes 221192 | tf_op jit(solution)/shard_map/ppermute | solution.py:561
  18.5 0.0 copy-start
  18.5 0.0 copy-start.1
  18.5 5.8 %basis.1.refs_4_ = bf16[18,2,2,256,256]{4,3,2,1,0:T(8,128)(2,1)S(1)} custom-call(s32[1,128]{1,0:T(1,128)S(1)} %get-tuple-element.30.refs_0_.refs_6_, f32[8,256]{1,0:T(8,128)S(1)} %get-tuple-element.31.refs_1_, f32[48,128]{1,0:T(8,128)S(1)} %get-tuple-element.32.refs_2_), custom_call_target="tpu_custom_call" | custom-call | flops 60000000 | bytes 1000000 | tf_op jit(solution)/shard_map/basis/pallas_call | solution.py:563
  24.3 0.0 collective-permute-done.2.refs_3_.refs_4_
  24.3 0.9 %collective-permute-done.1.refs_2_ = f32[144,128]{1,0:T(8,128)S(1)} collective-permute-done((f32[144,128]{1,0:T(8,128)S(1)}, f32[144,128]{1,0:T(8,128)S(1)}, u32[]{:S(2)}, u32[]{:S(2)}) %collective-permute-start.1) | collective-permute-done | bytes 73760 | tf_op jit(solution)/shard_map/ppermute | solution.py:561
  25.2 0.0 collective-permute-done.refs_1_.refs_5_
  25.2 6.7 %legendre.1 = f32[96,256]{1,0:T(8,128)S(1)} custom-call(f32[144,128]{1,0:T(8,128)S(1)} %get-tuple-element.29.refs_0_, f32[144,128]{1,0:T(8,128)S(1)} %collective-permute-done.refs_1_.refs_5_, f32[144,128]{1,0:T(8,128)S(1)} %collective-permute-done.1.refs_2_, f32[144,128]{1,0:T(8,128)S(1)} %collective-permute-done.2.refs_3_.refs_4_, ...), custom_call_target="tpu_custom_call" | custom-call | tf_op jit(solution)/shard_map/legendre/pallas_call | solution.py:580
  31.9 10.4 %all_gather.11.refs_0_ = f32[768,256]{1,0:T(8,128)S(1)} all-gather(f32[96,256]{1,0:T(8,128)S(1)} %legendre.1), channel_id=1, replica_groups=mesh['gy'=4,'gx'=8] {'gx'}, dimensions={0}, use_global_device_ids=true | all-gather | bytes 884736 | tf_op jit(solution)/shard_map/all_gather | solution.py:598
  42.3 0.0 copy-done
  42.3 0.0 copy-done.1
  42.3 2.1 %finish.1 = (f32[48,128]{1,0:T(8,128)}, f32[48,128]{1,0:T(8,128)}, f32[48,128]{1,0:T(8,128)}, f32[48,128]{1,0:T(8,128)}) custom-call(f32[768,256]{1,0:T(8,128)S(1)} %all_gather.11.refs_0_, f32[8,8,768]{2,1,0:T(8,128)S(1)} %copy-done.1, f32[2,104,768]{2,1,0:T(8,128)S(1)} %copy-done, s32[8]{0:T(128)S(1)} %get-tuple-element.28.refs_8_.refs_3_, ...), custom_call_target="tpu_custom_call" | custom-call | tf_op jit(solution)/shard_map/finish/pallas_call | solution.py:601
Async XLA Ops:
  13.9 10.5 %collective-permute-start.2 = (f32[144,128]{1,0:T(8,128)S(1)}, f32[144,128]{1,0:T(8,128)S(1)}, u32[]{:S(2)}, u32[]{:S(2)}) collective-permute-start(f32[144,128]{1,0:T(8,128)S(1)} %get-tuple-element.29.refs_0_), channel_id=1, source_target_pairs={{0,24},{8,0},{16,8},{24,16},{1,25},{9,1},{17,9},{25,17},{2,26},{10... | collective-permute-start | bytes 221192 | tf_op jit(solution)/shard_map/ppermute | solution.py:561
  17.5 7.7 %collective-permute-start.1 = (f32[144,128]{1,0:T(8,128)S(1)}, f32[144,128]{1,0:T(8,128)S(1)}, u32[]{:S(2)}, u32[]{:S(2)}) collective-permute-start(f32[144,128]{1,0:T(8,128)S(1)} %get-tuple-element.29.refs_0_), channel_id=1, source_target_pairs={{0,16},{8,24},{16,0},{24,8},{1,17},{9,25},{17,1},{25,9},{2,18},{10... | collective-permute-start | bytes 221192 | tf_op jit(solution)/shard_map/ppermute | solution.py:561
  17.5 7.7 %collective-permute-start = (f32[144,128]{1,0:T(8,128)S(1)}, f32[144,128]{1,0:T(8,128)S(1)}, u32[]{:S(2)}, u32[]{:S(2)}) collective-permute-start(f32[144,128]{1,0:T(8,128)S(1)} %get-tuple-element.29.refs_0_), channel_id=1, source_target_pairs={{0,8},{8,16},{16,24},{24,0},{1,9},{9,17},{17,25},{25,1},{2,10},{10... | collective-permute-start | bytes 221192 | tf_op jit(solution)/shard_map/ppermute | solution.py:561
  18.5 23.7 %copy-start = (f32[2,104,768]{2,1,0:T(8,128)S(1)}, f32[2,104,768]{2,1,0:T(8,128)}, u32[]{:S(2)}) copy-start(f32[2,104,768]{2,1,0:T(8,128)} %constant.23.clone.refs_2_) | copy-start | bytes 1916932
  18.5 23.7 %copy-start.1 = (f32[8,8,768]{2,1,0:T(8,128)S(1)}, f32[8,8,768]{2,1,0:T(8,128)}, u32[]{:S(2)}) copy-start(f32[8,8,768]{2,1,0:T(8,128)} %constant.22.clone.refs_1_) | copy-start | bytes 589828

commit v3 on v2

--- a/solution.py
+++ b/solution.py
@@ -14,7 +14,7 @@
 STEPS = 32
 ROWS = GROUP * STEPS
 CHAINS = 2
-UNROLL = 2
+UNROLL = 3
 EDGE = 8
 F32 = jnp.float32
 BF16 = jnp.bfloat16
@@ -53,7 +53,6 @@
         longest = max(-(-sum(counts) // CHAINS) for counts in lists)
         longest = max(longest, max(max(counts) for counts in lists))
         self.n_iter = -(-longest // UNROLL) * UNROLL
-        idle = -(-self.degrees // STEPS)
         per_row = self.n_iter * CHAINS * 2
         self.sched_width = -(-per_row // 128) * 128
         self.sched = np.zeros((self.n_gx, 1, self.sched_width), np.int32)
@@ -68,22 +67,22 @@
                     second += [(s, k) for k in range(head)]
                     first += [(s, k) for k in range(head, count)]
                     room = 0
-            last = max(range(self.n_slots), key=lambda s: counts[s])
             for chain in (first, second):
                 while len(chain) < self.n_iter:
-                    chain.append((self.n_slots, idle))
+                    chain.append((self.n_slots, 0))
             for i in range(self.n_iter):
                 for h, chain in enumerate((first, second)):
                     at = (i * CHAINS + h) * 2
                     self.sched[c, 0, at : at + 2] = chain[i]
-        self.love_width = -(-(self.degrees + GROUP * self.n_gx * (self.n_slots + 1) + STEPS * (idle + 1)) // 128) * 128
+        top = self.n_gx * (self.n_slots + 1) * GROUP
+        self.love_width = -(-(max(top, self.degrees) + 2 * STEPS) // 128) * 128
 
     def _tables(self):
-        rows = np.arange(self.half)
+        rows = np.arange(self.nlat).reshape(2, self.half)
         theta = np.pi * (rows + 0.5) / self.nlat
-        self.geo = np.zeros((8, self.half), np.float32)
-        self.geo[0] = np.cos(theta)
-        self.geo[1] = np.log(np.sin(theta))
+        self.geo = np.zeros((2, 8, self.half), np.float32)
+        self.geo[:, 0] = np.cos(theta)
+        self.geo[:, 1] = np.log(np.sin(theta))
         all_theta = np.pi * (np.arange(self.nlat) + 0.5) / self.nlat
         quad = np.pi / self.nlat * (2.0 * np.pi / self.nlon) * np.sin(all_theta)
         self.quad = np.repeat(
@@ -141,6 +140,24 @@
     )
 
 
+def dot3(a, b):
+    a_hi, b_hi = a.astype(BF16), b.astype(BF16)
+    a_lo = (a - a_hi.astype(F32)).astype(BF16)
+    b_lo = (b - b_hi.astype(F32)).astype(BF16)
+    n = a.shape[0]
+    dims = (((1,), (0,)), ((), ()))
+    both = jnp.concatenate([a_hi, a_lo], axis=0)
+    big = lax.dot_general(both, b_hi, dims, preferred_element_type=F32)
+    small = lax.dot_general(a_hi, b_lo, dims, preferred_element_type=F32)
+    return big[:n] + (big[n:] + small)
+
+
+def rows_of(tile, size):
+    height = tile.shape[0]
+    tile = jnp.concatenate([tile, jnp.zeros((size - height, size), F32)], axis=0)
+    return tile.T[:EDGE, :]
+
+
 def flip_matrix(size, flipped):
     row = iota((size, size), 0)
     col = iota((size, size), 1)
@@ -167,6 +184,8 @@
             source = source.at[c]
         elif k in SLICED_GY:
             source = source.at[r]
+        elif k in SLICED_HALF:
+            source = source.at[jnp.where(r < plan.n_gy // 2, 0, 1)]
         copies.append(pltpu.make_async_copy(source, target, sem.at[k]))
     for copy in copies:
         copy.start()
@@ -183,20 +202,20 @@
     out[lon + 2 : lon + 3, :] = depth_v[lon - 1 :, :]
     out[lon + 3 : lon + 4, :] = wet[lon - 1 :, :]
     out[lon + 4 : lon + 5, :] = east_v[lon - 1 :, :]
-    out[lon + 5 : lon + EDGE, :] = jnp.zeros((EDGE - 5, lat), F32)
     lane = iota((lon, lat), 1)
-    out[lon + EDGE :, :] = jnp.where(
-        lane == 0, depth_v[:, lat - 1 :], jnp.where(lane == 1, wet[:, lat - 1 :], 0.0)
-    )
+    tile = jnp.zeros((lon, lat), F32)
+    for k, array in enumerate([depth_v, wet, surface]):
+        tile = jnp.where(lane == k, array[:, lat - 1 :], tile)
+    out[lon + 5 :, :] = rows_of(tile, lat)[: EDGE - 5]
     for copy in copies[4:]:
         copy.wait()
 
 
-def fourier_kernel(
-    plan, gathered, u, v, quad, surface, depth, mask, north, fold_v, out, edges, fold, sem
-):
+def fourier_kernel(plan, *refs):
+    gathered, u, v, quad, surface, depth, mask, north, fold_v = refs[:9]
+    n_gx, n_gy, slots = plan.n_gx, plan.n_gy, plan.n_slots
+    outs, edges, fold, sem = refs[9 : 9 + n_gy], *refs[9 + n_gy :]
     lon, lat = plan.tile_lon, plan.tile_lat
-    n_gx, slots = plan.n_gx, plan.n_slots
     c, r = here()
     fetch = pltpu.make_async_copy(fold_v, fold, sem)
     fetch.start()
@@ -209,17 +228,21 @@
         cos_rows.append(uc * vc - us * vs)
         sin_rows.append(us * vc + uc * vs)
     trig = jnp.concatenate(cos_rows + sin_rows, axis=0)
-    sums = dot(trig, field) * quad[:1, :]
-    out[lon:, :] = dot(sums, flip_matrix(lat, r >= plan.n_gy // 2))
+    sums = dot3(trig, field) * quad[:1, :]
+    flipped = dot3(sums, flip_matrix(lat, True))
     wet = mask[...].astype(F32)
     lane = iota((lon, lat), 1)
     tile = jnp.zeros((lon, lat), F32)
-    last = [surface, depth, wet, north]
-    for k, array in enumerate(last):
+    for k, array in enumerate([surface, depth, wet, north]):
         tile = jnp.where(lane == k, array[:, lat - 1 :], tile)
     for k, array in enumerate([surface, depth, wet]):
         tile = jnp.where(lane == 4 + k, array[:, :1], tile)
-    out[:lon, :] = tile
+    halo = rows_of(tile, lat)
+    for k in range(n_gy):
+        target = lax.rem(r + k, n_gy)
+        same = (r < n_gy // 2) == (target < n_gy // 2)
+        outs[k][:EDGE, :] = halo
+        outs[k][EDGE:, :] = jnp.where(same, sums, flipped)
     after = lax.rem(c + 1, n_gx)
     before = lax.rem(c + n_gx - 1, n_gx)
     fetch.wait()
@@ -229,10 +252,12 @@
     edges[3:4, :] = gathered[before, lon - 1 : lon, :]
     edges[4:7, :] = gathered[before, lon + 2 : lon + 5, :]
     edges[7:8, :] = jnp.zeros((1, lat), F32)
-    across = jnp.where(
-        lane == 2, gathered[partner, :lon, lat - 1 :], gathered[partner, lon + EDGE :, :]
-    )
-    edges[EDGE:, :] = dot(flip_matrix(lon, True), across)
+    across = jnp.concatenate(
+        [gathered[partner, lon + 5 : lon + EDGE, :], jnp.zeros((5, lat), F32)], axis=0
+    )
+    i, j = iota((lat, lat), 0), iota((lat, lat), 1)
+    back = jnp.where((i < lon) & (i + j == lon - 1), 1.0, 0.0).astype(F32)
+    edges[EDGE:, :] = dot(across, back)
 
 
 def scheduled(plan, c, sched, i, h):
@@ -243,7 +268,7 @@
     return slot, chunk, group
 
 
-def basis_kernel(plan, sched_v, geo, seed_logs, p_out, seeds, unscale, state, sched, sem):
+def basis_kernel(plan, sched_v, geo, seed_logs, p_out, unscale, seeds, state, sched, sem):
     slots, half = plan.n_slots, plan.half
     c, _ = here()
     fetch = pltpu.make_async_copy(sched_v, sched, sem)
@@ -267,8 +292,8 @@
     lane_c = iota((GROUP, 128), 1)
     fetch.wait()
 
-    def begin(i, h):
-        slot, chunk, group = scheduled(plan, c, sched, i, h)
+    def coefficients(i, h):
+        _, chunk, group = scheduled(plan, c, sched, i, h)
         m0 = group * GROUP
         degree = (m0 + chunk * STEPS + lane_c).astype(F32)
         order = (m0 + sub_c).astype(F32)
@@ -281,24 +306,30 @@
             jnp.maximum(below * below - order * order, 0.0)
             / jnp.maximum(4.0 * below * below - 1.0, 1.0)
         )
+        return growth, growth * damping
+
+    def begin(i, h):
+        slot, chunk, _ = scheduled(plan, c, sched, i, h)
         started = jnp.where(chunk == 0, 0.0, 1.0).astype(F32)
         seed = seeds[slot] * (1.0 - started)
-        return slot, growth, growth * damping, seed, unscale[slot], state[slot, 0], state[slot, 1]
+        return slot, seed, state[slot, 0], state[slot, 1]
 
     def body(i, carry):
         lanes = [begin(i, h) for h in range(CHAINS)]
-        previous = [lane[5] for lane in lanes]
-        before = [lane[6] for lane in lanes]
+        ahead = [coefficients(jnp.minimum(i + 1, plan.n_iter - 1), h) for h in range(CHAINS)]
+        previous = [lane[2] for lane in lanes]
+        before = [lane[3] for lane in lanes]
         pairs = [[] for _ in range(CHAINS)]
         for t in range(STEPS):
-            for h, (_, growth, fall, seed, scale, _, _) in enumerate(lanes):
+            for h, (_, seed, _, _) in enumerate(lanes):
+                growth, fall = carry[h]
                 a = jnp.broadcast_to(growth[:, t : t + 1], (GROUP, half))
                 b = jnp.broadcast_to(fall[:, t : t + 1], (GROUP, half))
                 value = (a * x) * previous[h] - b * before[h]
                 if t < GROUP:
                     value = value + jnp.where(sub == t, seed, 0.0)
                 previous[h], before[h] = value, previous[h]
-                pairs[h].append(value * scale)
+                pairs[h].append(value)
                 if t % 2 == 1:
                     both = jnp.concatenate(pairs[h], axis=0)
                     both_hi = both.astype(BF16)
@@ -311,28 +342,29 @@
         for h, lane in enumerate(lanes):
             state[lane[0], 0] = previous[h]
             state[lane[0], 1] = before[h]
-        return carry
-
-    lax.fori_loop(0, plan.n_iter, body, 0)
+        return tuple(ahead)
+
+    lax.fori_loop(0, plan.n_iter, body, tuple(coefficients(0, h) for h in range(CHAINS)))
 
 
 def legendre_kernel(plan, *refs):
     n_gy, slots, half = plan.n_gy, plan.n_slots, plan.half
     lon, lat, k_half = plan.tile_lon, plan.tile_lat, plan.k_dev // 2
     blocks = refs[:n_gy]
-    basis, love, sched_v, out = refs[n_gy : n_gy + 4]
-    (fabs, lhs, weights, shifted, acc, coeffs, north_b, south_b, sched, sem) = refs[n_gy + 4 :]
+    basis, unscale, love, sched_v, out = refs[n_gy : n_gy + 5]
+    (fabs, lhs, weights, acc, coeffs_a, coeffs_b, own_b, mirror_b, sched, sem) = refs[n_gy + 5 :]
     c, r = here()
     fetch = pltpu.make_async_copy(sched_v, sched, sem)
     fetch.start()
     n_half = n_gy // 2
     for k in range(n_gy):
-        fabs[lax.rem(r - k + n_gy, n_gy)] = blocks[k][lon:, :]
+        fabs[lax.rem(r - k + n_gy, n_gy)] = blocks[k][EDGE:, :]
+    first_row = jnp.where(r < n_half, 0, n_half)
     sym, anti = [], []
     for b in range(n_half):
-        north, south = fabs[b], fabs[n_gy - 1 - b]
-        sym.append(north + south)
-        anti.append(north - south)
+        near, far = fabs[first_row + b], fabs[n_gy - 1 - first_row - b]
+        sym.append(near + far)
+        anti.append(near - far)
     sym = jnp.concatenate(sym, axis=1)
     anti = jnp.concatenate(anti, axis=1)
     for s in range(slots):
@@ -341,105 +373,118 @@
             [sym[lo:hi], anti[lo:hi], sym[k_half + lo : k_half + hi], anti[k_half + lo : k_half + hi]],
             axis=0,
         )
+        rows = rows * jnp.concatenate([unscale[s]] * 4, axis=0)
         rows_hi = rows.astype(BF16)
         lhs[s, : 4 * GROUP, :] = rows_hi
         lhs[s, 4 * GROUP :, :] = (rows - rows_hi.astype(F32)).astype(BF16)
     acc[...] = jnp.zeros(acc.shape, F32)
     lhs[slots] = jnp.zeros((8 * GROUP, half), BF16)
-    padded = jnp.concatenate(
-        [love[...].reshape(1, -1), jnp.zeros((1, plan.love_width - plan.degrees), F32)], axis=1
-    )
-    padded = jnp.broadcast_to(padded, (8, plan.love_width))
     fetch.wait()
-    items = plan.n_iter * CHAINS
-    for item in range(items):
-        _, chunk, group = scheduled(plan, c, sched, item // CHAINS, item % CHAINS)
-        start = group * GROUP + chunk * STEPS
-        rolled = pltpu.roll(padded, plan.love_width - start, 1)
-        shifted[item : item + 1, :] = rolled[:1, :128]
-    spread = iota((128, ROWS), 1) // GROUP == iota((128, ROWS), 0)
-    weights[...] = dot(shifted[...], jnp.where(spread, 1.0, 0.0).astype(F32)).reshape(
-        items, 1, ROWS
-    )
     row = iota((4 * GROUP, ROWS), 0)
     lane = iota((4 * GROUP, ROWS), 1)
     i_row, i_lane, t_lane = row % GROUP, lane % GROUP, lane // GROUP
     keep = jnp.where(
         (i_row == i_lane) & ((t_lane + i_row) % 2 == (row // GROUP) % 2), 1.0, 0.0
     ).astype(F32)
+    starts = 128 // GROUP
     nt = (((1,), (1,)), ((), ()))
     nn = (((1,), (0,)), ((), ()))
     n = 4 * GROUP
 
-    def analyse(i, h):
-        slot, _, _ = scheduled(plan, c, sched, i, h)
-        left = lhs[slot]
+    def products(i, h):
+        left = lhs[scheduled(plan, c, sched, i, h)[0]]
         one = lax.dot_general(left, basis[i, h, 0], nt, preferred_element_type=F32)
         two = lax.dot_general(left[:n], basis[i, h, 1], nt, preferred_element_type=F32)
-        coeff = (one[:n] + one[n:] + two) * keep * weights[i * CHAINS + h]
+        return one[:n] + one[n:] + two
+
+    def coefficients(i, h, total):
+        _, chunk, group = scheduled(plan, c, sched, i, h)
+        begin = group + chunk * (STEPS // GROUP)
+        at = (begin // starts + 1) * starts - 1 - lax.rem(begin, starts)
+        coeff = total * keep * weights[at]
         coeff_hi = coeff.astype(BF16)
         coeff_lo = (coeff - coeff_hi.astype(F32)).astype(BF16)
         return jnp.concatenate([coeff_hi, coeff_lo], axis=0)
 
-    def synthesise(i, h):
-        right = coeffs[i, h]
+    def synthesise(i, h, right):
         three = lax.dot_general(right, basis[i, h, 0], nn, preferred_element_type=F32)
         four = lax.dot_general(right[:n], basis[i, h, 1], nn, preferred_element_type=F32)
         return three[:n] + three[n:] + four
 
-    def analyse_all(k):
+    def analyse_all(k, into):
         for j in range(UNROLL):
             for h in range(CHAINS):
                 i = k * UNROLL + j
-                coeffs[i, h] = analyse(i, h)
-
-    def synthesise_all(k):
-        found = [
-            (scheduled(plan, c, sched, k * UNROLL + j, h)[0], synthesise(k * UNROLL + j, h))
-            for j in range(UNROLL)
-            for h in range(CHAINS)
-        ]
-        return found
-
-    def accumulate(found):
+                into[j, h] = coefficients(i, h, products(i, h))
+
+    def synthesise_all(k, given):
+        found = []
+        for j in range(UNROLL):
+            for h in range(CHAINS):
+                i = k * UNROLL + j
+                slot = scheduled(plan, c, sched, i, h)[0]
+                found.append((slot, synthesise(i, h, given[j, h])))
         for slot, part in found:
             acc[slot] += part
 
-    trips = plan.n_iter // UNROLL
-    analyse_all(0)
-
-    def body(k, carry):
-        found = synthesise_all(k - 1)
-        analyse_all(k)
-        accumulate(found)
-        return carry
-
-    lax.fori_loop(1, trips, body, 0)
-    accumulate(synthesise_all(trips - 1))
+    stages = plan.n_iter // UNROLL
+    first = [[products(j, h) for h in range(CHAINS)] for j in range(UNROLL)]
+    width = plan.love_width
+    padded = jnp.concatenate(
+        [love[...].reshape(1, -1), jnp.zeros((1, width - plan.degrees), F32)], axis=1
+    )
+    shifted = pltpu.roll(
+        jnp.broadcast_to(padded, (starts, width)),
+        width - GROUP * (starts - 1), 1, stride=GROUP, stride_axis=0,
+    )
+    shifted = jnp.concatenate(
+        [shifted[:, k * 128 : (k + 1) * 128] for k in range(width // 128)], axis=0
+    )
+    spread = iota((128, ROWS), 1) // GROUP == iota((128, ROWS), 0)
+    weights[...] = dot(shifted, jnp.where(spread, 1.0, 0.0).astype(F32)).reshape(
+        weights.shape
+    )
+    for j in range(UNROLL):
+        for h in range(CHAINS):
+            coeffs_a[j, h] = coefficients(j, h, first[j][h])
+
+    trips = (stages - 1) // 2
+    for k in range(trips):
+        analyse_all(2 * k + 1, coeffs_b)
+        synthesise_all(2 * k, coeffs_a)
+        analyse_all(2 * k + 2, coeffs_a)
+        synthesise_all(2 * k + 1, coeffs_b)
+    if stages % 2 == 0:
+        analyse_all(stages - 1, coeffs_b)
+    synthesise_all(2 * trips, coeffs_a)
+    if stages % 2 == 0:
+        synthesise_all(stages - 1, coeffs_b)
 
     for s in range(slots):
         lo, hi = s * GROUP, (s + 1) * GROUP
-        g = acc[s]
+        g = acc[s] * jnp.concatenate([unscale[s]] * 4, axis=0)
         for part in range(2):
             even = g[2 * part * GROUP : (2 * part + 1) * GROUP]
             odd = g[(2 * part + 1) * GROUP : (2 * part + 2) * GROUP]
             for b in range(n_half):
                 lanes = slice(b * lat, (b + 1) * lat)
                 where = slice(part * k_half + lo, part * k_half + hi)
-                north_b[b, where, :] = even[:, lanes] + odd[:, lanes]
-                south_b[b, where, :] = even[:, lanes] - odd[:, lanes]
-    is_north = r < n_half
-    mine = jnp.where(is_north, r, n_gy - 1 - r)
-    own = jnp.where(is_north, north_b[mine], south_b[mine])
-    out[:, :lat] = dot(own, flip_matrix(lat, jnp.logical_not(is_north)))
-    up_n = jnp.minimum(r + 1, n_half - 1)
-    up_s = jnp.clip(n_gy - 2 - r, 0, n_half - 1)
-    up = jnp.where(r + 1 < n_half, north_b[up_n][:, :1], south_b[up_s][:, lat - 1 :])
-    down_n = jnp.clip(r - 1, 0, n_half - 1)
-    down_s = jnp.clip(n_gy - r, 0, n_half - 1)
-    down = jnp.where(r - 1 < n_half, north_b[down_n][:, lat - 1 :], south_b[down_s][:, :1])
-    lane_o = iota((plan.k_dev, lat), 1)
-    out[:, lat:] = jnp.where(lane_o == 0, up, jnp.where(lane_o == 1, down, 0.0))
+                own_b[b, where, :] = even[:, lanes] + odd[:, lanes]
+                mirror_b[b, where, :] = even[:, lanes] - odd[:, lanes]
+    k_dev = plan.k_dev
+    mine = r - first_row
+    out[:k_dev, :] = own_b[mine]
+    up = jnp.where(
+        r == n_half - 1,
+        mirror_b[mine][:, lat - 1 :],
+        own_b[jnp.minimum(mine + 1, n_half - 1)][:, :1],
+    )
+    down = jnp.where(
+        r == n_half, mirror_b[mine][:, :1], own_b[jnp.maximum(mine - 1, 0)][:, lat - 1 :]
+    )
+    lane_o = iota((k_dev, lat), 1)
+    columns = jnp.where(lane_o == 0, up, jnp.where(lane_o == 1, down, 0.0))
+    out[k_dev:, :] = rows_of(columns, lat)
 
 
 def finish_kernel(
@@ -458,16 +503,27 @@
     a_fold = a_table[fold[c]]
     fold_trig = a_fold[0:1, :] * b_table[0, split:, :] + a_fold[1:2, :] * b_table[1, split:, :]
     trig = jnp.concatenate([own_trig, fold_trig], axis=0)
-    sal_all = dot(trig, terms[...])
+    k_dev, n_gx = plan.k_dev, plan.n_gx
+    main = jnp.concatenate([terms[d, :k_dev, :] for d in range(n_gx)], axis=0)
+    sal_all = dot3(trig, main)
+    up = jnp.concatenate([terms[d, k_dev : k_dev + 1, :k_dev] for d in range(n_gx)], axis=1)
+    down = jnp.concatenate([terms[d, k_dev + 1 : k_dev + 2, :k_dev] for d in range(n_gx)], axis=1)
+    sal_up = jnp.sum(trig[:lon] * up, axis=1, keepdims=True)
+    sal_down = jnp.sum(trig[:lon] * down, axis=1, keepdims=True)
     sal = sal_all[:lon, :lat]
     sal_out[...] = sal
     is_top = r == plan.n_gy - 1
-    sal_n = jnp.where(is_top, sal_all[split:, lat - 1 : lat], sal_all[:lon, lat : lat + 1])
-    sal_s = sal_all[:lon, lat + 1 : lat + 2]
+    sal_n = jnp.where(is_top, sal_all[split:, lat - 1 :], sal_up)
+    sal_s = sal_down
     surface, depth = surface_ref[...], depth_ref[...]
     wet = mask[...].astype(F32)
     east, north = east_ref[...], north_ref[...]
-    across = edges[EDGE:, :]
+    turned = jnp.concatenate(
+        [north_tile[:EDGE, :], south_tile[:EDGE, :], edges[EDGE:, :],
+         jnp.zeros((lat - 3 * EDGE, lat), F32)], axis=0,
+    ).T[:lon, :]
+    north_tile, south_tile = turned[:, :EDGE], turned[:, EDGE : 2 * EDGE]
+    across = turned[:, 2 * EDGE : 3 * EDGE]
     surf_n = jnp.where(is_top, across[:, 2:3], north_tile[:lon, 4:5])
     depth_n = jnp.where(is_top, across[:, 0:1], north_tile[:lon, 5:6])
     wet_n = jnp.where(is_top, across[:, 1:2], north_tile[:lon, 6:7])
@@ -511,6 +567,7 @@
 HBM = pl.BlockSpec(memory_space=pltpu.HBM)
 SLICED_GX = (5, 10)
 SLICED_GY = (7,)
+SLICED_HALF = (8,)
 
 
 def on_device(height, east_speed, north_speed, water_depth, ocean_mask, fold_partner, love_factor):
@@ -518,7 +575,7 @@
     n_gx, n_gy = lax.axis_size("gx"), lax.axis_size("gy")
     plan = Plan(lon, lat, n_gx, n_gy, love_factor.shape[0])
     slots, half = plan.n_slots, plan.half
-    sent = 2 * lon + EDGE
+    sent = lon + EDGE
     sources = (
         height, ocean_mask, water_depth, east_speed, north_speed, plan.u_table, plan.v_table,
         plan.quad, plan.geo, plan.seed_logs, plan.sched, love_factor, fold_partner,
@@ -527,7 +584,7 @@
         pltpu.with_memory_space_constraint(jnp.asarray(source), pltpu.HBM) for source in sources
     )
     kept_shapes = [
-        source.shape[1:] if k in SLICED_GX + SLICED_GY else source.shape
+        source.shape[1:] if k in SLICED_GX + SLICED_GY + SLICED_HALF else source.shape
         for k, source in enumerate(sources)
     ]
     kept = [
@@ -544,29 +601,34 @@
     )(*sources)
     mask, depth, east, north, u, v, quad, geo, seed_logs, sched, love, fold = kept
     gathered = lax.all_gather(packed, "gx", axis=0, tiled=False)
-    rows = lon + plan.k_dev
+    rows = EDGE + plan.k_dev
     fold_scratch = [pltpu.SMEM((n_gx,), jnp.int32), pltpu.SemaphoreType.DMA]
-    mine, edges = pl.pallas_call(
+    *messages, edges = pl.pallas_call(
         lambda *refs: fourier_kernel(plan, *refs),
         in_specs=[VMEM] * 9,
-        out_specs=[VMEM] * 2,
-        out_shape=(pltpu.VMEM((rows, lat), F32), pltpu.VMEM((lon + EDGE, lat), F32)),
+        out_specs=[VMEM] * (n_gy + 1),
+        out_shape=(
+            *[pltpu.VMEM((rows, lat), F32) for _ in range(n_gy)],
+            pltpu.VMEM((2 * EDGE, lat), F32),
+        ),
         scratch_shapes=fold_scratch,
         compiler_params=PARAMS,
         name="fourier",
     )(gathered, u, v, quad, surface, depth, mask, north, fold)
-    blocks = [mine]
+    blocks = [messages[0]]
     for k in range(1, n_gy):
         ring = [(i, (i + k) % n_gy) for i in range(n_gy)]
-        blocks.append(lax.ppermute(mine, "gy", ring))
+        blocks.append(lax.ppermute(messages[k], "gy", ring))
     sched_scratch = [pltpu.SMEM((1, plan.sched_width), jnp.int32), pltpu.SemaphoreType.DMA]
-    basis = pl.pallas_call(
+    basis, unscale = pl.pallas_call(
         lambda *refs: basis_kernel(plan, *refs),
         in_specs=[VMEM] * 3,
-        out_specs=VMEM,
-        out_shape=pltpu.VMEM((plan.n_iter, CHAINS, 2, ROWS, half), BF16),
+        out_specs=[VMEM] * 2,
+        out_shape=(
+            pltpu.VMEM((plan.n_iter, CHAINS, 2, ROWS, half), BF16),
+            pltpu.VMEM((slots + 1, GROUP, half), F32),
+        ),
         scratch_shapes=[
-            pltpu.VMEM((slots + 1, GROUP, half), F32),
             pltpu.VMEM((slots + 1, GROUP, half), F32),
             pltpu.VMEM((slots + 1, 2, GROUP, half), F32),
         ]
@@ -575,27 +637,26 @@
         compiler_params=PARAMS,
         name="basis",
     )(sched, geo, seed_logs)
-    items = plan.n_iter * CHAINS
     split_shape = pltpu.VMEM((n_gy // 2, plan.k_dev, lat), F32)
     terms = pl.pallas_call(
         lambda *refs: legendre_kernel(plan, *refs),
-        in_specs=[VMEM] * (n_gy + 3),
+        in_specs=[VMEM] * (n_gy + 4),
         out_specs=VMEM,
-        out_shape=pltpu.VMEM((plan.k_dev, 2 * lat), F32),
+        out_shape=pltpu.VMEM((plan.k_dev + EDGE, lat), F32),
         scratch_shapes=[
             pltpu.VMEM((n_gy, plan.k_dev, lat), F32),
             pltpu.VMEM((slots + 1, 8 * GROUP, half), BF16),
-            pltpu.VMEM((items, 1, ROWS), F32),
-            pltpu.VMEM((items, 128), F32),
+            pltpu.VMEM((plan.love_width // GROUP, 1, ROWS), F32),
             pltpu.VMEM((slots + 1, 4 * GROUP, half), F32),
-            pltpu.VMEM((plan.n_iter, CHAINS, 8 * GROUP, ROWS), BF16),
+            pltpu.VMEM((UNROLL, CHAINS, 8 * GROUP, ROWS), BF16),
+            pltpu.VMEM((UNROLL, CHAINS, 8 * GROUP, ROWS), BF16),
             split_shape, split_shape,
         ]
         + sched_scratch,
         compiler_params=PARAMS,
         name="legendre",
-    )(*blocks, basis, love, sched)
-    everything = lax.all_gather(terms, "gx", axis=0, tiled=True)
+    )(*blocks, basis, unscale, love, sched)
+    everything = lax.all_gather(terms, "gx", axis=0, tiled=False)
     tile = jax.ShapeDtypeStruct((lon, lat), F32)
     a_table, b_table = jnp.asarray(plan.a_table), jnp.asarray(plan.b_table)
     return pl.pallas_call(

time: 44.6 us -> 41.2 us (0.924)
  Pallas kernels: 16.6 us -> 14.2 us
  blocking collectives: 21.6 us -> 20.5 us
  starting transfers between devices: 4.66 us -> 5.57 us
  waiting for transfers between devices: 0.87 us -> 0.01 us
    pallas_call x1, Pallas kernels: 6.67 us -> 5.18 us  [on_device(): pl.pallas_call(lambda *refs: legendre_kernel(plan, *refs), in_specs=[VMEM...]
    ppermute x3, starting transfers between devices: 4.66 us -> 5.57 us  [on_device(): blocks.append(lax.ppermute(messages[k], 'gy', ring))]
    ppermute x3, waiting for transfers between devices: 0.87 us -> 0.01 us  [on_device(): blocks.append(lax.ppermute(messages[k], 'gy', ring))]
    all_gather x1, blocking collectives: 10.4 us -> 9.68 us  [on_device(): everything = lax.all_gather(terms, 'gx', axis=0, tiled=False)]
    pallas_call x1, Pallas kernels: 5.79 us -> 5.24 us  [on_device(): pl.pallas_call(lambda *refs: basis_kernel(plan, *refs), in_specs=[VMEM] *...]
  transfers between devices with their start and end apart: 3 -> 3, of which waited for: 1 -> 0; matrix products, arithmetic and copies ran while one was open for 0% -> 0% of each run, Pallas kernels for 13% -> 13%
where the time goes in v3:
time: 41.2 us; the launch traced here: 41 us
  blocking collectives  20.5 us (50%)
  Pallas kernels  14.2 us (34%)
  starting transfers between devices  5.57 us (14%)
  between operations  0.71 us (2%)
    all_gather x1, blocking collectives, on_device(): gathered = lax.all_gather(packed, 'gx', axis=0, tiled=False)  10.8 us
    all_gather x1, blocking collectives, on_device(): everything = lax.all_gather(terms, 'gx', axis=0, tiled=False)  9.68 us
    ppermute x3, starting transfers between devices, on_device(): blocks.append(lax.ppermute(messages[k], 'gy', ring))  5.57 us
    pallas_call x1, Pallas kernels, on_device(): pl.pallas_call(lambda *refs: basis_kernel(plan, *refs), in_specs=[VMEM] *...  5.24 us
    pallas_call x1, Pallas kernels, on_device(): pl.pallas_call(lambda *refs: legendre_kernel(plan, *refs), in_specs=[VMEM...  5.18 us
    pallas_call x1, Pallas kernels, on_device(): pl.pallas_call(lambda *refs: finish_kernel(plan, *refs), in_specs=[VMEM]...  1.77 us
    pallas_call x1, Pallas kernels, on_device(): pl.pallas_call(lambda *refs: pack_kernel(plan, *refs), in_specs=[HBM] * l...  1.15 us
    pallas_call x1, Pallas kernels, on_device(): pl.pallas_call(lambda *refs: fourier_kernel(plan, *refs), in_specs=[VMEM]...  0.91 us
  transfers between devices with their start and end apart: 3, of which 0 were waited for; matrix products, arithmetic and copies ran while one was open for 0% of the time, Pallas kernels for 13%

profile of v3, /device:TPU:0, one launch (start us, length us, event | category | flops | bytes accessed | tf_op | source)
XLA Modules:
  0.0 41.0 jit_solution(6655425013122195394)
XLA Ops:
  0.6 0.0 copy-start
  0.6 0.0 copy-start.1
  0.7 1.1 %pack.1 = (f32[56,128]{1,0:T(8,128)S(1)}, f32[48,128]{1,0:T(8,128)S(1)}, s32[48,128]{1,0:T(8,128)S(1)}, f32[48,128]{1,0:T(8,128)S(1)}, f32[48,128]{1,0:T(8,128)S...) custom-call(f32[48,128]{1,0:T(8,128)} %refs_0_.1, ...), custom_call_target="tpu_custom_call" | custom-call | tf_op jit(solution)/shard_map/pack/pallas_call | solution.py:593
  1.8 10.8 %all-gather = f32[448,128]{1,0:T(8,128)S(1)} all-gather(f32[56,128]{1,0:T(8,128)S(1)} %get-tuple-element.25), channel_id=2, replica_groups=mesh['gy'=4,'gx'=8] {'gx'}, dimensions={0}, use_global_device_ids=true | all-gather | bytes 258048 | tf_op jit(solution)/shard_map/all_gather | solution.py:603
  12.6 0.9 %fourier.1 = (f32[104,128]{1,0:T(8,128)S(1)}, f32[104,128]{1,0:T(8,128)S(1)}, f32[104,128]{1,0:T(8,128)S(1)}, f32[104,128]{1,0:T(8,128)S(1)}, f32[16,128]{1,0:T(8,128)S(1)}) custom-call(f32[8,56,128]{2,1,0:T(8,128)S(1)} %bitcast.3, f32[16,384]{1,0:T(8,128)S(1)} %get-tuple-element.26.refs_1_, f32[16,384]{1,0:T(8,128)S(1)} %get-tuple-element.27.refs_2_, ...), custom_call_target="tpu_custom_call" | custom-call | tf_op jit(solution)/shard_map/fourier/pallas_call | solution.py:606
  13.5 1.6 %collective-permute-start = (f32[104,128]{1,0:T(8,128)S(1)}, f32[104,128]{1,0:T(8,128)S(1)}, u32[]{:S(2)}, u32[]{:S(2)}) collective-permute-start(f32[104,128]{1,0:T(8,128)S(1)} %get-tuple-element.35), channel_id=1, source_target_pairs={{0,8},{8,16},{16,24},{24,0},{1,9},{9,17},{17,25},{25,1},{2,10},{10... | collective-permute-start | bytes 159752 | tf_op jit(solution)/shard_map/ppermute | solution.py:621
  15.1 2.6 %collective-permute-start.1 = (f32[104,128]{1,0:T(8,128)S(1)}, f32[104,128]{1,0:T(8,128)S(1)}, u32[]{:S(2)}, u32[]{:S(2)}) collective-permute-start(f32[104,128]{1,0:T(8,128)S(1)} %get-tuple-element.36), channel_id=1, source_target_pairs={{0,16},{8,24},{16,0},{24,8},{1,17},{9,25},{17,1},{25,9},{2,18},{10... | collective-permute-start | bytes 159752 | tf_op jit(solution)/shard_map/ppermute | solution.py:621
  17.7 1.4 %collective-permute-start.2 = (f32[104,128]{1,0:T(8,128)S(1)}, f32[104,128]{1,0:T(8,128)S(1)}, u32[]{:S(2)}, u32[]{:S(2)}) collective-permute-start(f32[104,128]{1,0:T(8,128)S(1)} %get-tuple-element.37), channel_id=1, source_target_pairs={{0,24},{8,0},{16,8},{24,16},{1,25},{9,1},{17,9},{25,17},{2,26},{10... | collective-permute-start | bytes 159752 | tf_op jit(solution)/shard_map/ppermute | solution.py:621
  19.1 5.2 %basis.1 = (bf16[18,2,2,256,256]{4,3,2,1,0:T(8,128)(2,1)S(1)}, f32[7,8,256]{2,1,0:T(8,128)S(1)}) custom-call(s32[1,128]{1,0:T(1,128)S(1)} %get-tuple-element.38.refs_0_.refs_7_, f32[8,256]{1,0:T(8,128)S(1)} %get-tuple-element.39.refs_1_, f32[48,128]{1,0:T(8,128)S(1)} %get-tuple-element.40.refs_2_), custom_call_target="tpu_custom_call" | custom-call | flops 60000000 | bytes 1000000 | tf_op jit(solution)/shard_map/basis/pallas_call | solution.py:623
  24.3 0.0 collective-permute-done.refs_1_.refs_5_
  24.3 0.0 collective-permute-done.1.refs_2_
  24.4 0.0 collective-permute-done.2.refs_3_.refs_4_
  24.4 5.2 %legendre.1 = f32[104,128]{1,0:T(8,128)S(1)} custom-call(f32[104,128]{1,0:T(8,128)S(1)} %get-tuple-element.34.refs_0_, f32[104,128]{1,0:T(8,128)S(1)} %collective-permute-done.refs_1_.refs_5_, f32[104,128]{1,0:T(8,128)S(1)} %collective-permute-done.1.refs_2_, f32[104,128]{1,0:T(8,128)S(1)} %collective-permute-done.2.refs_3_.refs_4_, ...), custom_call_target="tpu_custom_call" | custom-call | tf_op jit(solution)/shard_map/legendre/pallas_call | solution.py:641
  29.5 9.7 %all-gather.1 = f32[832,128]{1,0:T(8,128)S(1)} all-gather(f32[104,128]{1,0:T(8,128)S(1)} %legendre.1), channel_id=3, replica_groups=mesh['gy'=4,'gx'=8] {'gx'}, dimensions={0}, use_global_device_ids=true | all-gather | bytes 479232 | tf_op jit(solution)/shard_map/all_gather | solution.py:659
  39.2 0.0 copy-done
  39.2 0.0 copy-done.1
  39.2 1.8 %finish.1 = (f32[48,128]{1,0:T(8,128)}, f32[48,128]{1,0:T(8,128)}, f32[48,128]{1,0:T(8,128)}, f32[48,128]{1,0:T(8,128)}) custom-call(f32[8,104,128]{2,1,0:T(8,128)S(1)} %bitcast.2, f32[8,8,768]{2,1,0:T(8,128)S(1)} %copy-done.1, f32[2,104,768]{2,1,0:T(8,128)S(1)} %copy-done, s32[8]{0:T(128)S(1)} %get-tuple-element.33.refs_8_.refs_3_, ...), custom_call_target="tpu_custom_call" | custom-call | tf_op jit(solution)/shard_map/finish/pallas_call | solution.py:662
Async XLA Ops:
  0.6 38.6 %copy-start = (f32[2,104,768]{2,1,0:T(8,128)S(1)}, f32[2,104,768]{2,1,0:T(8,128)}, u32[]{:S(2)}) copy-start(f32[2,104,768]{2,1,0:T(8,128)} %constant.23.clone.refs_2_) | copy-start | bytes 1916932
  0.6 38.6 %copy-start.1 = (f32[8,8,768]{2,1,0:T(8,128)S(1)}, f32[8,8,768]{2,1,0:T(8,128)}, u32[]{:S(2)}) copy-start(f32[8,8,768]{2,1,0:T(8,128)} %constant.22.clone.refs_1_) | copy-start | bytes 589828
  13.5 10.8 %collective-permute-start = (f32[104,128]{1,0:T(8,128)S(1)}, f32[104,128]{1,0:T(8,128)S(1)}, u32[]{:S(2)}, u32[]{:S(2)}) collective-permute-start(f32[104,128]{1,0:T(8,128)S(1)} %get-tuple-element.35), channel_id=1, source_target_pairs={{0,8},{8,16},{16,24},{24,0},{1,9},{9,17},{17,25},{25,1},{2,10},{10... | collective-permute-start | bytes 159752 | tf_op jit(solution)/shard_map/ppermute | solution.py:621
  15.1 9.2 %collective-permute-start.1 = (f32[104,128]{1,0:T(8,128)S(1)}, f32[104,128]{1,0:T(8,128)S(1)}, u32[]{:S(2)}, u32[]{:S(2)}) collective-permute-start(f32[104,128]{1,0:T(8,128)S(1)} %get-tuple-element.36), channel_id=1, source_target_pairs={{0,16},{8,24},{16,0},{24,8},{1,17},{9,25},{17,1},{25,9},{2,18},{10... | collective-permute-start | bytes 159752 | tf_op jit(solution)/shard_map/ppermute | solution.py:621
  17.7 6.6 %collective-permute-start.2 = (f32[104,128]{1,0:T(8,128)S(1)}, f32[104,128]{1,0:T(8,128)S(1)}, u32[]{:S(2)}, u32[]{:S(2)}) collective-permute-start(f32[104,128]{1,0:T(8,128)S(1)} %get-tuple-element.37), channel_id=1, source_target_pairs={{0,24},{8,0},{16,8},{24,16},{1,25},{9,1},{17,9},{25,17},{2,26},{10... | collective-permute-start | bytes 159752 | tf_op jit(solution)/shard_map/ppermute | solution.py:621

commit v4 on v3

--- a/solution.py
+++ b/solution.py
@@ -13,8 +13,8 @@
 GROUP = 8
 STEPS = 32
 ROWS = GROUP * STEPS
-CHAINS = 2
-UNROLL = 3
+CHAINS = 3
+UNROLL = 2
 EDGE = 8
 F32 = jnp.float32
 BF16 = jnp.bfloat16
@@ -57,23 +57,22 @@
         self.sched_width = -(-per_row // 128) * 128
         self.sched = np.zeros((self.n_gx, 1, self.sched_width), np.int32)
         for c, counts in enumerate(lists):
-            first, second, room = [], [], self.n_iter
+            chains, room = [[]], self.n_iter
             for s, count in enumerate(counts):
                 if room >= count:
-                    first += [(s, k) for k in range(count)]
+                    chains[-1] += [(s, k) for k in range(count)]
                     room -= count
                 else:
                     head = count - room
-                    second += [(s, k) for k in range(head)]
-                    first += [(s, k) for k in range(head, count)]
-                    room = 0
-            for chain in (first, second):
-                while len(chain) < self.n_iter:
-                    chain.append((self.n_slots, 0))
-            for i in range(self.n_iter):
-                for h, chain in enumerate((first, second)):
+                    chains[-1] += [(s, k) for k in range(head, count)]
+                    chains.append([(s, k) for k in range(head)])
+                    room = self.n_iter - head
+            chains += [[] for _ in range(CHAINS - len(chains))]
+            for h, chain in enumerate(chains):
+                chain += [(self.n_slots, 0)] * (self.n_iter - len(chain))
+                for i, item in enumerate(chain):
                     at = (i * CHAINS + h) * 2
-                    self.sched[c, 0, at : at + 2] = chain[i]
+                    self.sched[c, 0, at : at + 2] = item
         top = self.n_gx * (self.n_slots + 1) * GROUP
         self.love_width = -(-(max(top, self.degrees) + 2 * STEPS) // 128) * 128
 
@@ -268,11 +267,18 @@
     return slot, chunk, group
 
 
-def basis_kernel(plan, sched_v, geo, seed_logs, p_out, unscale, seeds, state, sched, sem):
+def basis_kernel(
+    plan, sched_v, geo, seed_logs, fold_v, a_table, p_out, unscale, a_own, a_fold,
+    seeds, state, sched, fold, sem,
+):
     slots, half = plan.n_slots, plan.half
     c, _ = here()
-    fetch = pltpu.make_async_copy(sched_v, sched, sem)
+    fetch = pltpu.make_async_copy(sched_v, sched, sem.at[0])
     fetch.start()
+    fetch_fold = pltpu.make_async_copy(fold_v, fold, sem.at[1])
+    fetch_fold.start()
+    fetch_own = pltpu.make_async_copy(a_table.at[c], a_own, sem.at[2])
+    fetch_own.start()
     log_sin = geo[1:2, :]
     sub = iota((GROUP, half), 0)
     pick = iota(seed_logs.shape, 1) == c
@@ -291,6 +297,9 @@
     sub_c = iota((GROUP, 128), 0)
     lane_c = iota((GROUP, 128), 1)
     fetch.wait()
+    fetch_fold.wait()
+    fetch_across = pltpu.make_async_copy(a_table.at[fold[c]], a_fold, sem.at[1])
+    fetch_across.start()
 
     def coefficients(i, h):
         _, chunk, group = scheduled(plan, c, sched, i, h)
@@ -334,10 +343,11 @@
                     both = jnp.concatenate(pairs[h], axis=0)
                     both_hi = both.astype(BF16)
                     at = (t - 1) * GROUP
-                    p_out[i, h, 0, at : at + 2 * GROUP, :] = both_hi
-                    p_out[i, h, 1, at : at + 2 * GROUP, :] = (
-                        both - both_hi.astype(F32)
-                    ).astype(BF16)
+                    both_lo = (both - both_hi.astype(F32)).astype(BF16)
+                    for k in range(half // 128):
+                        lanes_k = slice(k * 128, (k + 1) * 128)
+                        p_out[i, h, 0, k, at : at + 2 * GROUP, :] = both_hi[:, lanes_k]
+                        p_out[i, h, 1, k, at : at + 2 * GROUP, :] = both_lo[:, lanes_k]
                     pairs[h] = []
         for h, lane in enumerate(lanes):
             state[lane[0], 0] = previous[h]
@@ -345,6 +355,8 @@
         return tuple(ahead)
 
     lax.fori_loop(0, plan.n_iter, body, tuple(coefficients(0, h) for h in range(CHAINS)))
+    fetch_own.wait()
+    fetch_across.wait()
 
 
 def legendre_kernel(plan, *refs):
@@ -352,7 +364,7 @@
     lon, lat, k_half = plan.tile_lon, plan.tile_lat, plan.k_dev // 2
     blocks = refs[:n_gy]
     basis, unscale, love, sched_v, out = refs[n_gy : n_gy + 5]
-    (fabs, lhs, weights, acc, coeffs_a, coeffs_b, own_b, mirror_b, sched, sem) = refs[n_gy + 5 :]
+    (fabs, lhs, weights, acc, coeffs_a, coeffs_b, own_b, mirror_b, turned, sched, sem) = refs[n_gy + 5 :]
     c, r = here()
     fetch = pltpu.make_async_copy(sched_v, sched, sem)
     fetch.start()
@@ -391,10 +403,19 @@
     nn = (((1,), (0,)), ((), ()))
     n = 4 * GROUP
 
+    def matrix(i, h, part):
+        return jnp.concatenate([basis[i, h, part, k] for k in range(half // 128)], axis=1)
+
     def products(i, h):
         left = lhs[scheduled(plan, c, sched, i, h)[0]]
-        one = lax.dot_general(left, basis[i, h, 0], nt, preferred_element_type=F32)
-        two = lax.dot_general(left[:n], basis[i, h, 1], nt, preferred_element_type=F32)
+        at = (i % (2 * UNROLL)) * CHAINS + h
+        turned[at, 0] = matrix(i, h, 0).T
+        one = lax.dot_general(left, turned[at, 0], nn, preferred_element_type=F32)
+        if i < UNROLL:
+            two = lax.dot_general(left[:n], matrix(i, h, 1), nt, preferred_element_type=F32)
+        else:
+            turned[at, 1] = matrix(i, h, 1).T
+            two = lax.dot_general(left[:n], turned[at, 1], nn, preferred_element_type=F32)
         return one[:n] + one[n:] + two
 
     def coefficients(i, h, total):
@@ -407,8 +428,8 @@
         return jnp.concatenate([coeff_hi, coeff_lo], axis=0)
 
     def synthesise(i, h, right):
-        three = lax.dot_general(right, basis[i, h, 0], nn, preferred_element_type=F32)
-        four = lax.dot_general(right[:n], basis[i, h, 1], nn, preferred_element_type=F32)
+        three = lax.dot_general(right, matrix(i, h, 0), nn, preferred_element_type=F32)
+        four = lax.dot_general(right[:n], matrix(i, h, 1), nn, preferred_element_type=F32)
         return three[:n] + three[n:] + four
 
     def analyse_all(k, into):
@@ -488,19 +509,14 @@
 
 
 def finish_kernel(
-    plan, terms, a_table, b_table, fold_v, north_tile, south_tile, edges,
+    plan, terms, a_own, a_fold, b_table, north_tile, south_tile, edges,
     surface_ref, depth_ref, mask, east_ref, north_ref,
-    sal_out, east_out, north_out, height_out, fold, sem,
+    sal_out, east_out, north_out, height_out,
 ):
     lon, lat = plan.tile_lon, plan.tile_lat
-    c, r = here()
-    fetch = pltpu.make_async_copy(fold_v, fold, sem)
-    fetch.start()
+    _, r = here()
     split = lon + EDGE
-    a_own = a_table[c]
     own_trig = a_own[0:1, :] * b_table[0, :split, :] + a_own[1:2, :] * b_table[1, :split, :]
-    fetch.wait()
-    a_fold = a_table[fold[c]]
     fold_trig = a_fold[0:1, :] * b_table[0, split:, :] + a_fold[1:2, :] * b_table[1, split:, :]
     trig = jnp.concatenate([own_trig, fold_trig], axis=0)
     k_dev, n_gx = plan.k_dev, plan.n_gx
@@ -620,23 +636,28 @@
         ring = [(i, (i + k) % n_gy) for i in range(n_gy)]
         blocks.append(lax.ppermute(messages[k], "gy", ring))
     sched_scratch = [pltpu.SMEM((1, plan.sched_width), jnp.int32), pltpu.SemaphoreType.DMA]
-    basis, unscale = pl.pallas_call(
+    a_table = pltpu.with_memory_space_constraint(jnp.asarray(plan.a_table), pltpu.HBM)
+    basis, unscale, a_own, a_fold = pl.pallas_call(
         lambda *refs: basis_kernel(plan, *refs),
-        in_specs=[VMEM] * 3,
-        out_specs=[VMEM] * 2,
+        in_specs=[VMEM] * 4 + [HBM],
+        out_specs=[VMEM] * 4,
         out_shape=(
-            pltpu.VMEM((plan.n_iter, CHAINS, 2, ROWS, half), BF16),
+            pltpu.VMEM((plan.n_iter, CHAINS, 2, half // 128, ROWS, 128), BF16),
             pltpu.VMEM((slots + 1, GROUP, half), F32),
+            pltpu.VMEM((8, plan.k_all), F32),
+            pltpu.VMEM((8, plan.k_all), F32),
         ),
         scratch_shapes=[
             pltpu.VMEM((slots + 1, GROUP, half), F32),
             pltpu.VMEM((slots + 1, 2, GROUP, half), F32),
-        ]
-        + sched_scratch,
+            pltpu.SMEM((1, plan.sched_width), jnp.int32),
+            pltpu.SMEM((n_gx,), jnp.int32),
+            pltpu.SemaphoreType.DMA((3,)),
+        ],
         cost_estimate=pl.CostEstimate(flops=60_000_000, bytes_accessed=1_000_000, transcendentals=0),
         compiler_params=PARAMS,
         name="basis",
-    )(sched, geo, seed_logs)
+    )(sched, geo, seed_logs, fold, a_table)
     split_shape = pltpu.VMEM((n_gy // 2, plan.k_dev, lat), F32)
     terms = pl.pallas_call(
         lambda *refs: legendre_kernel(plan, *refs),
@@ -651,6 +672,7 @@
             pltpu.VMEM((UNROLL, CHAINS, 8 * GROUP, ROWS), BF16),
             pltpu.VMEM((UNROLL, CHAINS, 8 * GROUP, ROWS), BF16),
             split_shape, split_shape,
+            pltpu.VMEM((2 * UNROLL * CHAINS, 2, half, ROWS), BF16),
         ]
         + sched_scratch,
         compiler_params=PARAMS,
@@ -658,17 +680,16 @@
     )(*blocks, basis, unscale, love, sched)
     everything = lax.all_gather(terms, "gx", axis=0, tiled=False)
     tile = jax.ShapeDtypeStruct((lon, lat), F32)
-    a_table, b_table = jnp.asarray(plan.a_table), jnp.asarray(plan.b_table)
+    b_table = jnp.asarray(plan.b_table)
     return pl.pallas_call(
         lambda *refs: finish_kernel(plan, *refs),
         in_specs=[VMEM] * 12,
         out_specs=[VMEM] * 4,
         out_shape=(tile,) * 4,
-        scratch_shapes=fold_scratch,
         compiler_params=PARAMS,
         name="finish",
     )(
-        everything, a_table, b_table, fold, blocks[n_gy - 1], blocks[1], edges,
+        everything, a_own, a_fold, b_table, blocks[n_gy - 1], blocks[1], edges,
         surface, depth, mask, east, north,
     )
 

time: 41.2 us -> 38.6 us (0.937)
  Pallas kernels: 14.2 us -> 11.6 us
    pallas_call x1, Pallas kernels: 5.18 us -> 3.83 us  [on_device(): pl.pallas_call(lambda *refs: legendre_kernel(plan, *refs), in_specs=[VMEM...]
    pallas_call x1, Pallas kernels: 5.24 us -> 4.52 us  [on_device(): pl.pallas_call(lambda *refs: basis_kernel(plan, *refs), in_specs=[VMEM] *...]
    pallas_call x1, Pallas kernels: 1.77 us -> 1.23 us  [on_device(): pl.pallas_call(lambda *refs: finish_kernel(plan, *refs), in_specs=[VMEM]...]
  transfers between devices with their start and end apart: 3 -> 3, of which waited for: 0 -> 0; matrix products, arithmetic and copies ran while one was open for 0% -> 0% of each run, Pallas kernels for 13% -> 12%
where the time goes in v4:
time: 38.6 us; the launch traced here: 38.4 us
  blocking collectives  20.5 us (53%)
  Pallas kernels  11.6 us (30%)
  starting transfers between devices  5.56 us (14%)
  between operations  0.7 us (2%)
    all_gather x1, blocking collectives, on_device(): gathered = lax.all_gather(packed, 'gx', axis=0, tiled=False)  10.8 us
    all_gather x1, blocking collectives, on_device(): everything = lax.all_gather(terms, 'gx', axis=0, tiled=False)  9.69 us
    ppermute x3, starting transfers between devices, on_device(): blocks.append(lax.ppermute(messages[k], 'gy', ring))  5.56 us
    pallas_call x1, Pallas kernels, on_device(): pl.pallas_call(lambda *refs: basis_kernel(plan, *refs), in_specs=[VMEM] *...  4.52 us
    pallas_call x1, Pallas kernels, on_device(): pl.pallas_call(lambda *refs: legendre_kernel(plan, *refs), in_specs=[VMEM...  3.83 us
    pallas_call x1, Pallas kernels, on_device(): pl.pallas_call(lambda *refs: finish_kernel(plan, *refs), in_specs=[VMEM]...  1.23 us
    pallas_call x1, Pallas kernels, on_device(): pl.pallas_call(lambda *refs: pack_kernel(plan, *refs), in_specs=[HBM] * l...  1.14 us
    pallas_call x1, Pallas kernels, on_device(): pl.pallas_call(lambda *refs: fourier_kernel(plan, *refs), in_specs=[VMEM]...  0.91 us
  transfers between devices with their start and end apart: 3, of which 0 were waited for; matrix products, arithmetic and copies ran while one was open for 0% of the time, Pallas kernels for 12%

profile of v4, /device:TPU:0, one launch (start us, length us, event | category | flops | bytes accessed | tf_op | source)
XLA Modules:
  0.0 38.4 jit_solution(12982555672454216034)
XLA Ops:
  0.6 0.0 copy-start
  0.6 1.1 %pack.1 = (f32[56,128]{1,0:T(8,128)S(1)}, f32[48,128]{1,0:T(8,128)S(1)}, s32[48,128]{1,0:T(8,128)S(1)}, f32[48,128]{1,0:T(8,128)S(1)}, f32[48,128]{1,0:T(8,128)S...) custom-call(f32[48,128]{1,0:T(8,128)} %refs_0_.1, ...), custom_call_target="tpu_custom_call" | custom-call | tf_op jit(solution)/shard_map/pack/pallas_call | solution.py:609
  1.8 10.8 %all-gather = f32[448,128]{1,0:T(8,128)S(1)} all-gather(f32[56,128]{1,0:T(8,128)S(1)} %get-tuple-element.27), channel_id=2, replica_groups=mesh['gy'=4,'gx'=8] {'gx'}, dimensions={0}, use_global_device_ids=true | all-gather | bytes 258048 | tf_op jit(solution)/shard_map/all_gather | solution.py:619
  12.6 0.9 %fourier.1 = (f32[104,128]{1,0:T(8,128)S(1)}, f32[104,128]{1,0:T(8,128)S(1)}, f32[104,128]{1,0:T(8,128)S(1)}, f32[104,128]{1,0:T(8,128)S(1)}, f32[16,128]{1,0:T(8,128)S(1)}) custom-call(f32[8,56,128]{2,1,0:T(8,128)S(1)} %bitcast.3, f32[16,384]{1,0:T(8,128)S(1)} %get-tuple-element.28.refs_1_, f32[16,384]{1,0:T(8,128)S(1)} %get-tuple-element.29.refs_2_, ...), custom_call_target="tpu_custom_call" | custom-call | tf_op jit(solution)/shard_map/fourier/pallas_call | solution.py:622
  13.5 1.6 %collective-permute-start = (f32[104,128]{1,0:T(8,128)S(1)}, f32[104,128]{1,0:T(8,128)S(1)}, u32[]{:S(2)}, u32[]{:S(2)}) collective-permute-start(f32[104,128]{1,0:T(8,128)S(1)} %get-tuple-element.37), channel_id=1, source_target_pairs={{0,8},{8,16},{16,24},{24,0},{1,9},{9,17},{17,25},{25,1},{2,10},{10... | collective-permute-start | bytes 159752 | tf_op jit(solution)/shard_map/ppermute | solution.py:637
  15.1 2.6 %collective-permute-start.1 = (f32[104,128]{1,0:T(8,128)S(1)}, f32[104,128]{1,0:T(8,128)S(1)}, u32[]{:S(2)}, u32[]{:S(2)}) collective-permute-start(f32[104,128]{1,0:T(8,128)S(1)} %get-tuple-element.38), channel_id=1, source_target_pairs={{0,16},{8,24},{16,0},{24,8},{1,17},{9,25},{17,1},{25,9},{2,18},{10... | collective-permute-start | bytes 159752 | tf_op jit(solution)/shard_map/ppermute | solution.py:637
  17.7 1.3 %collective-permute-start.2 = (f32[104,128]{1,0:T(8,128)S(1)}, f32[104,128]{1,0:T(8,128)S(1)}, u32[]{:S(2)}, u32[]{:S(2)}) collective-permute-start(f32[104,128]{1,0:T(8,128)S(1)} %get-tuple-element.39), channel_id=1, source_target_pairs={{0,24},{8,0},{16,8},{24,16},{1,25},{9,1},{17,9},{25,17},{2,26},{10... | collective-permute-start | bytes 159752 | tf_op jit(solution)/shard_map/ppermute | solution.py:637
  19.1 4.5 %basis.1 = (bf16[12,3,2,2,256,128]{5,4,3,2,1,0:T(8,128)(2,1)S(1)}, f32[7,8,256]{2,1,0:T(8,128)S(1)}, f32[8,768]{1,0:T(8,128)S(1)}, f32[8,768]{1,0:T(8,128)S(1)}) custom-call(s32[1,128]{1,0:T(1,128)S(1)} %get-tuple-element.40.refs_0_.refs_7_, f32[8,256]{1,0:T(8,128)S(1)} %get-tuple-element.41.refs_1_, f32[48,128]{1,0:T(8,128)S(1)} %get-tuple-element.42.refs_2_, ...), custom_call_target="tpu_custom_call" | custom-call | flops 60000000 | bytes 1000000 | tf_op jit(solution)/shard_map/basis/pallas_call | solution.py:640
  23.6 0.0 collective-permute-done.refs_1_.refs_5_
  23.6 0.0 collective-permute-done.1.refs_2_
  23.6 0.0 collective-permute-done.2.refs_3_.refs_4_
  23.6 3.8 %legendre.1 = f32[104,128]{1,0:T(8,128)S(1)} custom-call(f32[104,128]{1,0:T(8,128)S(1)} %get-tuple-element.36.refs_0_, f32[104,128]{1,0:T(8,128)S(1)} %collective-permute-done.refs_1_.refs_5_, f32[104,128]{1,0:T(8,128)S(1)} %collective-permute-done.1.refs_2_, f32[104,128]{1,0:T(8,128)S(1)} %collective-permute-done.2.refs_3_.refs_4_, ...), custom_call_target="tpu_custom_call" | custom-call | tf_op jit(solution)/shard_map/legendre/pallas_call | solution.py:662
  27.5 9.7 %all-gather.1 = f32[832,128]{1,0:T(8,128)S(1)} all-gather(f32[104,128]{1,0:T(8,128)S(1)} %legendre.1), channel_id=3, replica_groups=mesh['gy'=4,'gx'=8] {'gx'}, dimensions={0}, use_global_device_ids=true | all-gather | bytes 479232 | tf_op jit(solution)/shard_map/all_gather | solution.py:681
  37.2 0.0 copy-done
  37.2 1.2 %finish.1 = (f32[48,128]{1,0:T(8,128)}, f32[48,128]{1,0:T(8,128)}, f32[48,128]{1,0:T(8,128)}, f32[48,128]{1,0:T(8,128)}) custom-call(f32[8,104,128]{2,1,0:T(8,128)S(1)} %bitcast.2, f32[8,768]{1,0:T(8,128)S(1)} %get-tuple-element.46.refs_1_, f32[8,768]{1,0:T(8,128)S(1)} %get-tuple-element.47.refs_2_, f32[2,104,768]{2,1,0:T(8,128)S(1)} %copy-done, ...), custom_call_target="tpu_custom_call" | custom-call | tf_op jit(solution)/shard_map/finish/pallas_call | solution.py:684
Async XLA Ops:
  0.6 36.5 %copy-start = (f32[2,104,768]{2,1,0:T(8,128)S(1)}, f32[2,104,768]{2,1,0:T(8,128)}, u32[]{:S(2)}) copy-start(f32[2,104,768]{2,1,0:T(8,128)} %constant.23.clone.refs_3_) | copy-start | bytes 1916932
  13.5 10.1 %collective-permute-start = (f32[104,128]{1,0:T(8,128)S(1)}, f32[104,128]{1,0:T(8,128)S(1)}, u32[]{:S(2)}, u32[]{:S(2)}) collective-permute-start(f32[104,128]{1,0:T(8,128)S(1)} %get-tuple-element.37), channel_id=1, source_target_pairs={{0,8},{8,16},{16,24},{24,0},{1,9},{9,17},{17,25},{25,1},{2,10},{10... | collective-permute-start | bytes 159752 | tf_op jit(solution)/shard_map/ppermute | solution.py:637
  15.1 8.5 %collective-permute-start.1 = (f32[104,128]{1,0:T(8,128)S(1)}, f32[104,128]{1,0:T(8,128)S(1)}, u32[]{:S(2)}, u32[]{:S(2)}) collective-permute-start(f32[104,128]{1,0:T(8,128)S(1)} %get-tuple-element.38), channel_id=1, source_target_pairs={{0,16},{8,24},{16,0},{24,8},{1,17},{9,25},{17,1},{25,9},{2,18},{10... | collective-permute-start | bytes 159752 | tf_op jit(solution)/shard_map/ppermute | solution.py:637
  17.7 5.9 %collective-permute-start.2 = (f32[104,128]{1,0:T(8,128)S(1)}, f32[104,128]{1,0:T(8,128)S(1)}, u32[]{:S(2)}, u32[]{:S(2)}) collective-permute-start(f32[104,128]{1,0:T(8,128)S(1)} %get-tuple-element.39), channel_id=1, source_target_pairs={{0,24},{8,0},{16,8},{24,16},{1,25},{9,1},{17,9},{25,17},{2,26},{10... | collective-permute-start | bytes 159752 | tf_op jit(solution)/shard_map/ppermute | solution.py:637
